TPU v7x, 256 devices: a whole 4x4x8 slice. The times are simulated.
256 devices in a mesh: shot: 64 (over y, z, core), grp: 4 (over x).
Axes of the slice: x: 4, y: 4, z: 8, core: 2. Of those that a mesh axis runs over, the one named last changes fastest.
Arguments:
- offsets: bfloat16 [49152, 32, 512], P(('shot', 'grp')), may hold values from -500 to 500
- slant_weights: bfloat16 [64, 32], replicated, may hold values from -1 to 1
- live: int32 [49152, 64], P(('shot', 'grp')), may hold values from 0 to 1, as said below
- block_tile: int32 [24576, 1], P(('shot', 'grp')), may hold values from 0 to 63; in each aligned block of 96 rows (0 to 95, 96 to 191, ...) at most 2 rows name the same one
- image_slot: int32 [24576], P(('shot', 'grp')), may hold values from 0 to 15
Outputs:
- image: bfloat16 [1024, 128, 512], P(('shot', 'grp'))
Inputs may be any that keep to these rules, and one draw needn't show every extreme that they name: Each position's live angles are 0 up to a cutoff minus 1, the cutoff at least 16; the first position of every 192 positions keeps all 64 angles. `block_tile`: among the 96 blocks of one device no tile is named more than 2 times.
All inputs are finite; a program needn't handle non-finite values.
Results may differ from a plain program's by a relative error of at most 0.0049.
Values may be sent and summed in bfloat16 or wider, within the bound.
A program may use at most 192 MiB of HBM per device.

v0:
```python
import jax
import jax.numpy as jnp
from jax import lax
from jax.sharding import Mesh
from jax.sharding import PartitionSpec as P

IMG_DEV = 4
SHOT_GRP = ("shot_0", "shot_1", "shot_2", "grp")
SHOT = ("shot_0", "shot_1", "shot_2")


def over_axes(array, axes):
    for axis in axes:
        array = lax.psum(array, axis)
    return array


def in_blocks(array, dim, count):
    before, after = (array.shape[:dim], array.shape[dim + 1 :])
    return jnp.moveaxis(array.reshape(*before, count, -1, *after), dim, 0)


def sent_and_summed(array, axis, dim):
    parts = in_blocks(array, dim, lax.axis_size(axis))
    arrived = lax.all_to_all(parts, axis, split_axis=0, concat_axis=0, tiled=True)
    return arrived.sum(axis=0)


def slant_stack(gathers, weights, live_mask):
    slanted = jnp.einsum("ah,phz->paz", weights, gathers, preferred_element_type=jnp.float32)
    return (slanted * live_mask[:, :, None]).astype(jnp.bfloat16)


def angle_moments(angles, live_mask):
    widened = angles.astype(jnp.float32)
    return (jnp.sum(widened * widened, axis=(0, 2)), jnp.sum(live_mask, axis=0))


def global_gain(square_sum, live_count, depth_len):
    totals = (over_axes(square_sum, SHOT_GRP), over_axes(live_count, SHOT_GRP))
    return lax.rsqrt(totals[0] / (depth_len * totals[1]) + 1e-06)


def local(offsets, slant_weights, live, block_tile, image_slot):
    peer_count = lax.axis_size(SHOT)
    block_count = block_tile.shape[0]
    capacity = block_count // peer_count + 1
    slot_count = peer_count * capacity
    depth_len = offsets.shape[2]
    angle_count = slant_weights.shape[0]
    traces = 2 * angle_count
    tile_ids = block_tile[:, 0]
    block_index = jnp.arange(block_count)
    earlier = (tile_ids[:, None] == tile_ids[None, :]) & (
        block_index[None, :] < block_index[:, None]
    )
    slot_rank = jnp.sum(earlier.astype(jnp.int32), axis=1)
    targets = tile_ids * capacity + slot_rank
    labels = (
        jnp.full((slot_count,), -1.0, jnp.float32).at[targets].set(image_slot.astype(jnp.float32))
    )
    labels = labels.astype(jnp.bfloat16).reshape(peer_count, capacity)
    inner = offsets.shape[1:]
    raw_sent = (
        jnp.zeros((slot_count, 2) + inner, jnp.bfloat16)
        .at[targets]
        .set(offsets.reshape((block_count, 2) + inner))
    )
    live_sent = (
        jnp.zeros((slot_count, traces), jnp.bfloat16)
        .at[targets]
        .set(live.reshape(block_count, traces).astype(jnp.bfloat16))
    )
    raw_in, live_in, labels_in = (
        lax.all_to_all(
            raw_sent.reshape((peer_count, capacity, 2) + inner),
            SHOT,
            split_axis=0,
            concat_axis=0,
            tiled=True,
        ),
        lax.all_to_all(
            live_sent.reshape(peer_count, capacity, traces),
            SHOT,
            split_axis=0,
            concat_axis=0,
            tiled=True,
        ),
        lax.all_to_all(labels, SHOT, split_axis=0, concat_axis=0, tiled=True),
    )
    mask_in = live_in.reshape(slot_count * 2, angle_count).astype(jnp.float32)
    angles = slant_stack(raw_in.reshape((slot_count * 2,) + inner), slant_weights, mask_in)
    square_sum, live_count = angle_moments(angles, mask_in)
    received = angles.reshape(slot_count, traces * depth_len)
    angle_gain = global_gain(square_sum, live_count, depth_len)
    tile_rows = IMG_DEV * lax.axis_size("grp")
    slot_codes = labels_in.reshape(slot_count).astype(jnp.float32)
    holder = (slot_codes[None, :] == jnp.arange(tile_rows, dtype=jnp.float32)[:, None]).astype(
        jnp.bfloat16
    )
    stacked = sent_and_summed(
        jnp.dot(holder, received, preferred_element_type=jnp.float32), "grp", 0
    )
    trace_gain = jnp.tile(angle_gain, 2)
    return (stacked.reshape(IMG_DEV, traces, depth_len) * trace_gain[None, :, None]).astype(
        jnp.bfloat16
    )


def solution(mesh):
    torus = Mesh(
        mesh.devices.reshape(4, 8, 2, mesh.shape["grp"]), ("shot_0", "shot_1", "shot_2", "grp")
    )
    return jax.shard_map(
        local,
        mesh=torus,
        in_specs=(P(SHOT_GRP, None, None), P(), P(SHOT_GRP, None), P(SHOT_GRP, None), P(SHOT_GRP)),
        out_specs=P(SHOT_GRP, None, None),
        check_vma=False,
    )
```

profile of v0, /device:TPU:1, one launch (start us, length us, event | category | flops | bytes accessed | tf_op | source)
XLA Modules:
  0.0 352.6 jit_solution(17804898050667033546)
XLA Ops:
  0.0 0.0 copy-start
  0.0 0.9 convert_reduce_fusion
  0.9 0.7 fusion.10
  1.6 0.7 convert_element_type.49
  2.2 0.9 scatter_custom_fusion
  3.1 0.8 all_to_all.20
  3.9 13.1 %all-to-all-start = ((bf16[64,1,2]{2,1,0:T(2,128)(2,1)}), bf16[64,1,2]{2,1,0:T(2,128)(2,1)S(1)}, u32[]{:S(2)}, u32[]{:S(2)}) async-start(bf16[64,1,2]{2,1,0:T(2,128)(2,1)} %all_to_all.20), calls=%async_computation | async-start | bytes 65536 | tf_op jit(solution)/shard_map/all_to_all | solution.py:89
  17.1 0.8 convert_element_type.53
  17.9 0.1 copy.10
  18.0 0.1 reshape.92
  18.1 1.4 scatter_custom_fusion.2
  19.5 6.9 %all-to-all-done = bf16[64,1,2]{2,1,0:T(2,128)(2,1)S(1)} async-done(((bf16[64,1,2]{2,1,0:T(2,128)(2,1)}), bf16[64,1,2]{2,1,0:T(2,128)(2,1)S(1)}, u32[]{:S(2)}, u32[]{:S(2)}) %all-to-all-start) | async-done | bytes 288 | tf_op jit(solution)/shard_map/all_to_all | solution.py:89
  26.4 4.7 %all-to-all-start.2 = ((bf16[64,2,128]{2,1,0:T(2,128)(2,1)}), bf16[64,2,128]{2,1,0:T(2,128)(2,1)S(1)}, u32[]{:S(2)}, u32[]{:S(2)}) async-start(bf16[64,2,128]{2,1,0:T(2,128)(2,1)} %bitcast.7), calls=%async_computation.2 | async-start | bytes 65536 | tf_op jit(solution)/shard_map/all_to_all | solution.py:82
  31.1 4.3 %broadcast_in_dim.7 = bf16[128,2,32,512]{3,2,1,0:T(8,128)(2,1)} broadcast(bf16[]{:T(256)} %constant.5.clone.1), dimensions={} | broadcast | bytes 8388610 | tf_op jit(solution)/shard_map/broadcast_in_dim | solution.py:65
  35.4 17.7 %scatter_fusion = bf16[128,2,32,512]{3,2,1,0:T(8,128)(2,1)} fusion(bf16[128,2,32,512]{3,2,1,0:T(8,128)(2,1)} %broadcast_in_dim.7, s32[96]{0:T(128)S(1)} %fusion.10, bf16[96,2,32,512]{3,2,1,0:T(8,128)(2,1)} %bitcast.26), kind=kCustom, calls=%fused_computation.1 | custom fusion | bytes 18874752 | tf_op jit(solution)/shard_map/scatter | solution.py:67
  53.1 0.0 all-to-all-done.2
  53.1 10.5 %all-to-all-start.1 = ((bf16[64,2,2,32,512]{4,3,2,1,0:T(8,128)(2,1)}), bf16[64,2,2,32,512]{4,3,2,1,0:T(8,128)(2,1)}, u32[]{:S(2)}, u32[]{:S(2)}) async-start(bf16[64,2,2,32,512]{4,3,2,1,0:T(8,128)(2,1)} %bitcast.25), calls=%async_computation.1 | async-start | bytes 16777216 | tf_op jit(solution)/shard_map/all_to_all | solution.py:75
  63.6 0.1 convert_reduce_fusion.1
  63.7 0.1 reshape.70
  63.9 0.1 reshape.71
  63.9 185.4 %all-to-all-done.1 = bf16[64,2,2,32,512]{4,3,2,1,0:T(8,128)(2,1)} async-done(((bf16[64,2,2,32,512]{4,3,2,1,0:T(8,128)(2,1)}), bf16[64,2,2,32,512]{4,3,2,1,0:T(8,128)(2,1)}, u32[]{:S(2)}, u32[]{:S(2)}) %all-to-all-start.1) | async-done | bytes 8388640 | tf_op jit(solution)/shard_map/all_to_all | solution.py:75
  249.4 0.0 copy-done
  249.4 12.7 %multiply_reduce_fusion = (f32[64]{0:T(128)S(1)}, bf16[256,64,512]{2,1,0:T(8,128)(2,1)}) fusion(f32[256,64]{1,0:T(8,128)S(1)} %reshape.71, bf16[256,32,512]{2,1,0:T(8,128)(2,1)} %bitcast.5, bf16[64,32]{0,1:T(8,128)(2,1)S(1)} %copy-done), kind=kOutput, calls=%fused_computation.3 | convolution fusion | flops 578813888 | bytes 25235712 | tf_op jit(solution)/shard_map/ah,phz->paz/dot_general | solution.py:30
  262.0 20.4 %reshape.97 = bf16[128,65536,1]{1,0,2:T(8,128)(2,1)} reshape(bf16[256,64,512]{2,1,0:T(8,128)(2,1)} %get-tuple-element.14) | data formatting | bytes 33554432 | tf_op jit(solution)/shard_map/reshape | solution.py:94
  282.4 0.0 copy-start.1
  282.4 10.0 %fusion.6 = f32[4,4,65536]{2,1,0:T(4,128)} fusion(bf16[128,65536,1]{1,0,2:T(8,128)(2,1)} %reshape.97, f32[4,4]{1,0:T(4,128)S(1)} %multiply_add_fusion, f32[128]{0:T(128)S(1)} %reshape.70), kind=kOutput, calls=%fused_computation.15 | convolution fusion | flops 268437504 | bytes 20972096 | tf_op jit(solution)/shard_map/dot_general | solution.py:102
  292.5 4.8 %all-to-all-start.3 = ((f32[4,4,65536]{2,1,0:T(4,128)}), f32[4,4,65536]{2,1,0:T(4,128)}, u32[]{:S(2)}, u32[]{:S(2)}) async-start(f32[4,4,65536]{2,1,0:T(4,128)} %fusion.6), calls=%async_computation.3 | async-start | bytes 8388608 | tf_op jit(solution)/shard_map/all_to_all | solution.py:25
  297.3 0.1 reduce_sum.42
  297.4 9.4 %all-reduce.2 = (f32[64]{0:T(128)S(1)}, f32[64]{0:T(128)S(1)}) all-reduce(f32[64]{0:T(128)S(1)} %get-tuple-element.13, f32[64]{0:T(128)S(1)} %reduce_sum.42), channel_id=1, replica_groups=mesh['shot_0'=4,'shot_1'=8,'shot_2'=2,'grp'=4] {'shot_0'}, use_global_device_ids=true, to_apply=%region_6.0 | all-reduce | flops 128 | bytes 1024 | tf_op jit(solution)/shard_map/psum | solution.py:14
  306.8 12.6 %all-reduce = (f32[64]{0:T(128)S(1)}, f32[64]{0:T(128)S(1)}) all-reduce(f32[64]{0:T(128)S(1)} %get-tuple-element.9, f32[64]{0:T(128)S(1)} %get-tuple-element.10), channel_id=1, replica_groups=mesh['shot_0'=4,'shot_1'=8,'shot_2'=2,'grp'=4] {'shot_1'}, use_global_device_ids=true, to_apply=%region_7.0 | all-reduce | flops 128 | bytes 1024 | tf_op jit(solution)/shard_map/psum | solution.py:14
  319.4 5.3 %all-reduce.3 = (f32[64]{0:T(128)S(1)}, f32[64]{0:T(128)S(1)}) all-reduce(f32[64]{0:T(128)S(1)} %get-tuple-element.5, f32[64]{0:T(128)S(1)} %get-tuple-element.6), channel_id=1, replica_groups=mesh['shot_0'=4,'shot_1'=8,'shot_2'=2,'grp'=4] {'shot_2'}, use_global_device_ids=true, to_apply=%region_8.0 | all-reduce | flops 128 | bytes 1024 | tf_op jit(solution)/shard_map/psum | solution.py:14
  324.7 23.5 %all-reduce.1 = (f32[64]{0:T(128)S(1)}, f32[64]{0:T(128)S(1)}) all-reduce(f32[64]{0:T(128)S(1)} %get-tuple-element.11, f32[64]{0:T(128)S(1)} %get-tuple-element.12), channel_id=1, replica_groups=mesh['shot_0'=4,'shot_1'=8,'shot_2'=2,'grp'=4] {'grp'}, use_global_device_ids=true, to_apply=%region_9.0 | all-reduce | flops 128 | bytes 1024 | tf_op jit(solution)/shard_map/psum | solution.py:14
  348.2 0.1 mul.42
  348.2 0.0 all-to-all-done.3
  348.2 3.2 reduce_sum.40
  351.4 1.1 fusion.1
  352.6 0.0 copy-done.1
  (4 shorter events, 0.0 us)
Async XLA Ops:
  0.0 249.4 %copy-start = (bf16[64,32]{0,1:T(8,128)(2,1)S(1)}, bf16[64,32]{0,1:T(8,128)(2,1)}, u32[]{:S(2)}) copy-start(bf16[64,32]{0,1:T(8,128)(2,1)} %param.6) | copy-start | bytes 12292
  3.9 22.5 %all-to-all-start = ((bf16[64,1,2]{2,1,0:T(2,128)(2,1)}), bf16[64,1,2]{2,1,0:T(2,128)(2,1)S(1)}, u32[]{:S(2)}, u32[]{:S(2)}) async-start(bf16[64,1,2]{2,1,0:T(2,128)(2,1)} %all_to_all.20), calls=%async_computation | async-start | bytes 65536 | tf_op jit(solution)/shard_map/all_to_all | solution.py:89
  26.4 26.7 %all-to-all-start.2 = ((bf16[64,2,128]{2,1,0:T(2,128)(2,1)}), bf16[64,2,128]{2,1,0:T(2,128)(2,1)S(1)}, u32[]{:S(2)}, u32[]{:S(2)}) async-start(bf16[64,2,128]{2,1,0:T(2,128)(2,1)} %bitcast.7), calls=%async_computation.2 | async-start | bytes 65536 | tf_op jit(solution)/shard_map/all_to_all | solution.py:82
  53.1 196.3 %all-to-all-start.1 = ((bf16[64,2,2,32,512]{4,3,2,1,0:T(8,128)(2,1)}), bf16[64,2,2,32,512]{4,3,2,1,0:T(8,128)(2,1)}, u32[]{:S(2)}, u32[]{:S(2)}) async-start(bf16[64,2,2,32,512]{4,3,2,1,0:T(8,128)(2,1)} %bitcast.25), calls=%async_computation.1 | async-start | bytes 16777216 | tf_op jit(solution)/shard_map/all_to_all | solution.py:75
  282.4 70.1 %copy-start.1 = (bf16[64,32]{0,1:T(8,128)(2,1)S(1)}, bf16[64,32]{0,1:T(8,128)(2,1)}, u32[]{:S(2)}) copy-start(bf16[64,32]{0,1:T(8,128)(2,1)} %param.6) | copy-start | bytes 12292
  292.5 55.8 %all-to-all-start.3 = ((f32[4,4,65536]{2,1,0:T(4,128)}), f32[4,4,65536]{2,1,0:T(4,128)}, u32[]{:S(2)}, u32[]{:S(2)}) async-start(f32[4,4,65536]{2,1,0:T(4,128)} %fusion.6), calls=%async_computation.3 | async-start | bytes 8388608 | tf_op jit(solution)/shard_map/all_to_all | solution.py:25
where the time goes:
time: 354 us; the launch traced here: 353 us
  waiting for transfers between devices  192 us (54%)
  blocking collectives  50.8 us (14%)
  local copies, waits for them, and re-layouts  46 us (13%)
  starting transfers between devices  33.2 us (9%)
  matrix products  22.7 us (6%)
  other arithmetic  7.56 us (2%)
    all_to_all x1, waiting for transfers between devices, local(): lax.all_to_all(raw_sent.reshape((peer_count, capacity, 2) + inner), SHOT,...  185 us
    psum x4, blocking collectives, over_axes(): array = lax.psum(array, axis)  50.8 us
    reshape x1, local copies, waits for them, and re-layouts, local(): received = angles.reshape(slot_count, traces * depth_len)  20.4 us
    scatter x1, local copies, waits for them, and re-layouts, local(): raw_sent = jnp.zeros((slot_count, 2) + inner, jnp.bfloat16).at[targets].s...  17.7 us
    all_to_all x1, starting transfers between devices, local(): lax.all_to_all(labels, SHOT, split_axis=0, concat_axis=0, tiled=True)  13.1 us
    dot_general x1, matrix products, slant_stack(): jnp.einsum('ah,phz->paz', weights, gathers, preferred_element_type=jnp.fl...  12.7 us
    all_to_all x1, starting transfers between devices, local(): lax.all_to_all(raw_sent.reshape((peer_count, capacity, 2) + inner), SHOT,...  10.5 us
    dot_general x1, matrix products, local(): jnp.dot(holder, received, preferred_element_type=jnp.float32)  10 us
  transfers between devices with their start and end apart: 4, of which 2 were waited for; matrix products, arithmetic and copies ran while one was open for 7% of the time, Pallas kernels for 0%

commit v1 on v0

v1 whole, which is shorter than its diff:
```python
import functools

import jax
import jax.numpy as jnp
from jax import lax
from jax.experimental import pallas as pl
from jax.experimental.pallas import tpu as pltpu
from jax.sharding import Mesh
from jax.sharding import PartitionSpec as P

SHOT_GRP = ("y", "z", "c", "x")
SLAB = ("x", "y")
ANG = 64
LANES = 128
HALF = 64


def pack_body(low_ref, high_ref, out_ref):
    for quarter in range(4):
        for place in range(2):
            lanes = slice(quarter * LANES, (quarter + 1) * LANES)
            low = low_ref[:, place, :, lanes]
            high = high_ref[:, place, :, lanes]
            out_ref[quarter, 2 * place] = jnp.concatenate(
                [low[..., :HALF], high[..., :HALF]], axis=-1
            )
            out_ref[quarter, 2 * place + 1] = jnp.concatenate(
                [low[..., HALF:], high[..., HALF:]], axis=-1
            )


def packed(blocks):
    count, _, inner, depth = blocks.shape
    pairs, step = count // 2, 8
    return pl.pallas_call(
        pack_body,
        grid=(pairs // step,),
        in_specs=[
            pl.BlockSpec((step, 2, inner, depth), lambda i: (i, 0, 0, 0)),
            pl.BlockSpec((step, 2, inner, depth), lambda i: (i + pairs // step, 0, 0, 0)),
        ],
        out_specs=pl.BlockSpec((4, 4, step, inner, LANES), lambda i: (0, 0, i, 0, 0)),
        out_shape=jax.ShapeDtypeStruct((4, 4, pairs, inner, LANES), jnp.bfloat16),
        cost_estimate=pl.CostEstimate(
            flops=4 * blocks.size, bytes_accessed=4 * blocks.size, transcendentals=0
        ),
    )(blocks, blocks)


def square_body(step, cut_ref, raw_ref, weight_ref, out_ref):
    first = pl.program_id(0)

    @pl.when(first == 0)
    def _():
        out_ref[...] = jnp.zeros_like(out_ref)

    rows = lax.broadcasted_iota(jnp.int32, (ANG, LANES), 0)
    weights = weight_ref[...]
    total = jnp.zeros((ANG, LANES), jnp.float32)
    for i in range(step):
        angles = jnp.dot(weights, raw_ref[i], preferred_element_type=jnp.float32)
        squares = angles * angles
        folded = (squares[:, :128] + squares[:, 128:256]) + (
            squares[:, 256:384] + squares[:, 384:]
        )
        total += jnp.where(rows < cut_ref[first * step + i], folded, 0.0)
    out_ref[...] += total


def square_sums(offsets, weights, cuts):
    count, inner, depth = offsets.shape
    step = 16
    lanes = pl.pallas_call(
        functools.partial(square_body, step),
        grid_spec=pltpu.PrefetchScalarGridSpec(
            num_scalar_prefetch=1,
            grid=(count // step,),
            in_specs=[
                pl.BlockSpec((step, inner, depth), lambda i, cut: (i, 0, 0)),
                pl.BlockSpec((ANG, inner), lambda i, cut: (0, 0)),
            ],
            out_specs=pl.BlockSpec((ANG, LANES), lambda i, cut: (0, 0)),
        ),
        out_shape=jax.ShapeDtypeStruct((ANG, LANES), jnp.float32),
        cost_estimate=pl.CostEstimate(
            flops=2 * ANG * offsets.size, bytes_accessed=2 * offsets.size, transcendentals=0
        ),
    )(cuts, offsets, weights)
    return jnp.sum(lanes, axis=1)


def stack_body(pairs, code_ref, cut_ref, raw_ref, weight_ref, mine_ref, other_ref, acc_ref):
    source = pl.program_id(0)
    half = acc_ref.shape[0] // 2

    @pl.when(source == 0)
    def _():
        def clear(i, carry):
            acc_ref[pl.ds(i * 8, 8)] = jnp.zeros((8, ANG, LANES), jnp.float32)
            return carry

        lax.fori_loop(0, acc_ref.shape[0] // 8, clear, 0)

    rows = lax.broadcasted_iota(jnp.int32, (ANG, LANES), 0)
    weights = weight_ref[...]
    unroll = 8

    def group(i, carry):
        sides, places = [], []
        for u in range(unroll):
            row = raw_ref[0, i * unroll + u]
            zero = jnp.zeros((row.shape[0], HALF), jnp.bfloat16)
            left, right = row[:, :HALF], row[:, HALF:]
            for side, value in ((0, left), (1, right)):
                at = source * 2 * pairs + side * pairs + i * unroll + u
                code = code_ref[at]
                low = jnp.concatenate([value, zero], axis=1)
                high = jnp.concatenate([zero, value], axis=1)
                sides.append(jnp.where(code % 2 == 0, low, high))
                places.append((code // 2, cut_ref[at]))
        angles = jnp.dot(
            weights, jnp.concatenate(sides, axis=1), preferred_element_type=jnp.float32
        )
        for n, (place, cut) in enumerate(places):
            part = angles[:, n * LANES : (n + 1) * LANES]
            acc_ref[place] += jnp.where(rows < cut, part, 0.0)
        return carry

    lax.fori_loop(0, pairs // unroll, group, 0)

    @pl.when(source == pl.num_programs(0) - 1)
    def _():
        def put(i, carry):
            at = pl.ds(i * 8, 8)
            mine_ref[at] = acc_ref[at].astype(mine_ref.dtype)
            other_ref[at] = acc_ref[pl.ds(half + i * 8, 8)].astype(other_ref.dtype)
            return carry

        lax.fori_loop(0, half // 8, put, 0)


def stacked_parts(raw, weights, codes, cuts, places):
    sources, pairs, inner, _ = raw.shape
    shape = (places // 2, ANG, LANES)
    return pl.pallas_call(
        functools.partial(stack_body, pairs),
        grid_spec=pltpu.PrefetchScalarGridSpec(
            num_scalar_prefetch=2,
            grid=(sources,),
            in_specs=[
                pl.BlockSpec((1, pairs, inner, LANES), lambda i, a, b: (i, 0, 0, 0)),
                pl.BlockSpec((ANG, inner), lambda i, a, b: (0, 0)),
            ],
            out_specs=[pl.BlockSpec(shape, lambda i, a, b: (0, 0, 0))] * 2,
            scratch_shapes=[pltpu.VMEM((places, ANG, LANES), jnp.float32)],
        ),
        out_shape=[
            jax.ShapeDtypeStruct(shape, jnp.bfloat16),
            jax.ShapeDtypeStruct(shape, jnp.bfloat16),
        ],
        cost_estimate=pl.CostEstimate(
            flops=4 * ANG * raw.size, bytes_accessed=2 * raw.size, transcendentals=0
        ),
    )(codes, cuts, raw, weights)


def unpack_body(part_ref, out_ref):
    for quarter in range(4):
        for place in range(2):
            for pair in range(2):
                near = part_ref[4 * quarter + 2 * place, pair]
                far = part_ref[4 * quarter + 2 * place + 1, pair]
                at = (
                    slice(place * ANG, (place + 1) * ANG),
                    slice(quarter * LANES, (quarter + 1) * LANES),
                )
                out_ref[2 * pair, at[0], at[1]] = jnp.concatenate(
                    [near[:, :HALF], far[:, :HALF]], axis=1
                )
                out_ref[2 * pair + 1, at[0], at[1]] = jnp.concatenate(
                    [near[:, HALF:], far[:, HALF:]], axis=1
                )


def local(offsets, slant_weights, live, block_tile, image_slot):
    y, z, c = lax.axis_index("y"), lax.axis_index("z"), lax.axis_index("c")
    block_count = block_tile.shape[0]
    positions, inner, depth = offsets.shape
    tile = block_tile[:, 0]
    tile_y, tile_z, tile_c = tile // 16, tile // 2 % 8, tile % 2
    chunk = tile_z
    place = (tile_c ^ c) * 256 + chunk * 32 + image_slot // 4 * 8 + tile_y * 2
    code = (place + image_slot // 2 % 2) * 2 + image_slot % 2
    cuts = jnp.sum(live, axis=1)
    notes = jnp.concatenate([code, cuts])
    notes = lax.all_gather(notes, SLAB, axis=0, tiled=False)
    codes = notes[:, :block_count].reshape(-1)
    own_cuts = notes[:, block_count:].reshape(-1, block_count, 2)
    own_cuts = jnp.where(y // 2 == 0, own_cuts[..., 0], own_cuts[..., 1]).reshape(-1)

    sent = packed(offsets.reshape(block_count, 2, inner, depth))
    raw = lax.all_to_all(
        sent.reshape((16,) + sent.shape[2:]), SLAB, split_axis=0, concat_axis=0, tiled=True
    )
    squares = square_sums(offsets, slant_weights, cuts)
    counts = jnp.sum(live, axis=0).astype(jnp.float32)
    totals = lax.psum(jnp.stack([squares, counts]), SHOT_GRP)
    gain = lax.rsqrt(totals[0] / (depth * totals[1]) + 1e-06)

    mine, other = stacked_parts(raw, slant_weights, codes, own_cuts, 512)
    got = lax.ppermute(other, "c", [(0, 1), (1, 0)])
    both = (mine.astype(jnp.float32) + got.astype(jnp.float32)).astype(jnp.bfloat16)
    summed = lax.psum_scatter(
        both.reshape(8, 32, ANG, LANES), "z", scatter_dimension=0, tiled=False
    )
    scaled = (summed.astype(jnp.float32) * gain[None, :, None]).astype(jnp.bfloat16)
    parts = lax.all_to_all(
        scaled.reshape(16, 2, ANG, LANES), SLAB, split_axis=0, concat_axis=0, tiled=True
    )
    return pl.pallas_call(
        unpack_body,
        out_shape=jax.ShapeDtypeStruct((4, 2 * ANG, depth), jnp.bfloat16),
    )(parts)


def solution(mesh):
    torus = Mesh(mesh.devices.reshape(4, 8, 2, mesh.shape["grp"]), SHOT_GRP)
    return jax.shard_map(
        local,
        mesh=torus,
        in_specs=(P(SHOT_GRP, None, None), P(), P(SHOT_GRP, None), P(SHOT_GRP, None), P(SHOT_GRP)),
        out_specs=P(SHOT_GRP, None, None),
        check_vma=False,
    )
```

time: 354 us -> 358 us (1.011)
  blocking collectives: 50.8 us -> 243 us
  waiting for transfers between devices: 192 us -> 7.03 us
  Pallas kernels: 0 us -> 58.3 us
  local copies, waits for them, and re-layouts: 46 us -> 2.97 us
  matrix products: 22.7 us -> 0 us
  between operations: 0.1 us -> 14.2 us
  starting transfers between devices: 33.2 us -> 22.7 us
    all_to_all x4 -> x1, waiting for transfers between devices: 192 us -> 0.01 us  [local(): lax.all_to_all(sent.reshape((16,) + sent.shape[2:]), SLAB, split_axis=0,...]
    unnamed x0 -> x1, blocking collectives: none -> 151 us
    pallas_call x0 -> x4, Pallas kernels: none -> 58.3 us  [the longest x1 38 us: stacked_parts(): pl.pallas_call(functools.partial(stack_body, pairs), grid_spec=pltpu.Pref...]
    psum x4 -> x1, blocking collectives: 50.8 us -> 78.2 us  [local(): totals = lax.psum(jnp.stack([squares, counts]), SHOT_GRP)]
    all_to_all x4 -> x1, starting transfers between devices: 33.2 us -> 7.76 us  [local(): lax.all_to_all(sent.reshape((16,) + sent.shape[2:]), SLAB, split_axis=0,...]
    dot_general x2 -> x0, matrix products: 22.7 us -> none  [the longest x1 12.7 us: slant_stack(): jnp.einsum('ah,phz->paz', weights, gathers, preferred_element_type=jnp.fl...]
    scatter x3 -> x0, local copies, waits for them, and re-layouts: 20 us -> none  [the longest x1 17.7 us: local(): raw_sent = jnp.zeros((slot_count, 2) + inner, jnp.bfloat16).at[targets].s...]
    reshape x1, local copies, waits for them, and re-layouts: 20.4 us -> 0.67 us  [local(): codes = notes[:, :block_count].reshape(-1)]
  transfers between devices with their start and end apart: 4 -> 3, of which waited for: 2 -> 1; matrix products, arithmetic and copies ran while one was open for 7% -> 1% of each run, Pallas kernels for 0% -> 3%
where the time goes in v1:
time: 358 us; the launch traced here: 357 us
  blocking collectives  243 us (68%)
  Pallas kernels  58.3 us (16%)
  starting transfers between devices  22.7 us (6%)
  between operations  14.2 us (4%)
  other arithmetic  8.65 us (2%)
  waiting for transfers between devices  7.03 us (2%)
    unnamed x1, blocking collectives  151 us
    psum x1, blocking collectives, local(): totals = lax.psum(jnp.stack([squares, counts]), SHOT_GRP)  78.2 us
    pallas_call x1, Pallas kernels, stacked_parts(): pl.pallas_call(functools.partial(stack_body, pairs), grid_spec=pltpu.Pref...  38 us
    ppermute x1, starting transfers between devices, local(): got = lax.ppermute(other, 'c', [(0, 1), (1, 0)])  14.9 us
    all_to_all x1, blocking collectives, local(): lax.all_to_all(scaled.reshape(16, 2, ANG, LANES), SLAB, split_axis=0, con...  13.7 us
    pallas_call x1, Pallas kernels, square_sums(): pl.pallas_call(functools.partial(square_body, step), grid_spec=pltpu.Pref...  10.8 us
    all_to_all x1, starting transfers between devices, local(): lax.all_to_all(sent.reshape((16,) + sent.shape[2:]), SLAB, split_axis=0,...  7.76 us
    pallas_call x1, Pallas kernels, packed(): pl.pallas_call(pack_body, grid=(pairs // step,), in_specs=[pl.BlockSpec((...  7.51 us
  transfers between devices with their start and end apart: 3, of which 1 were waited for; matrix products, arithmetic and copies ran while one was open for 1% of the time, Pallas kernels for 3%

profile of v1, /device:TPU:1, one launch (start us, length us, event | category | flops | bytes accessed | tf_op | source)
XLA Modules:
  0.0 357.1 jit_solution(17648039466527035203)
XLA Ops:
  6.5 7.5 %shard_map.55 = bf16[4,4,48,32,128]{4,3,2,1,0:T(8,128)(2,1)} custom-call(bf16[96,2,32,512]{3,2,1,0:T(8,128)(2,1)} %bitcast.32, bf16[96,2,32,512]{3,2,1,0:T(8,128)(2,1)} %bitcast.33), custom_call_target="tpu_custom_call" | custom-call | flops 12582912 | bytes 12582912 | tf_op jit(solution)/shard_map/pallas_call | solution.py:35
  14.0 0.0 copy-start.5
  14.0 0.0 copy-start
  14.0 0.0 copy-start.3
  14.1 0.0 copy-start.4
  14.1 0.0 copy-start.2
  14.1 7.8 %all-to-all-start = ((bf16[16,48,32,128]{3,2,1,0:T(8,128)(2,1)}), bf16[16,48,32,128]{3,2,1,0:T(8,128)(2,1)}, u32[]{:S(2)}, u32[]{:S(2)}) async-start(bf16[16,48,32,128]{3,2,1,0:T(8,128)(2,1)} %bitcast.34), calls=%async_computation | async-start | bytes 12582912 | tf_op jit(solution)/shard_map/all_to_all | solution.py:202
  21.8 0.0 reduce-scatter.2.cloned.1.call-start
  21.9 0.0 copy-done.5
  21.9 0.6 dynamic-slice
  23.2 0.0 copy-done
  23.2 0.1 fusion.10
  23.3 0.0 copy-done.3
  23.3 0.0 copy-done.4
  23.3 0.0 copy-start.1
  23.3 0.2 add_dynamic-update-slice_fusion
  23.5 151.3 %all-reduce = s32[4608]{0:T(1024)S(1)} all-reduce(s32[4608]{0:T(1024)S(1)} %add_dynamic-update-slice_fusion), channel_id=2, replica_groups=mesh['y'=4,'z'=8,'c'=2,'x'=4] {'x','y'}, use_global_device_ids=true, to_apply=%add | all-reduce | flops 4608 | bytes 36864
  174.8 0.1 reshape.56
  174.9 0.1 slice.25
  175.0 0.0 copy-done.2
  175.0 0.7 copy.13.weight_ref
  175.7 0.7 reshape.50.code_ref
  176.3 0.1 copy.11
  176.4 0.1 broadcast_select_fusion
  176.5 0.1 copy.12
  176.6 0.7 select_n.60.cut_ref
  177.2 0.0 all-to-all-done.raw_ref
  177.2 38.0 %shard_map.56 = (bf16[256,64,128]{2,1,0:T(8,128)(2,1)}, bf16[256,64,128]{2,1,0:T(8,128)(2,1)}) custom-call(s32[1536]{0:T(1024)} %reshape.50.code_ref, s32[1536]{0:T(1024)} %select_n.60.cut_ref, bf16[16,48,32,128]{3,2,1,0:T(8,128)(2,1)} %all-to-all-done.raw_ref, bf16[64,32]{1,0:T(8,128)(2,1)} %copy.13.weight_ref), custom_call_target="tpu_custom_call" | custom-call | flops 805306368 | bytes 6291456 | tf_op jit(solution)/shard_map/pallas_call | solution.py:145
  215.2 14.9 %collective-permute-start = (bf16[256,64,128]{2,1,0:T(8,128)(2,1)}, bf16[256,64,128]{2,1,0:T(8,128)(2,1)S(1)}, u32[]{:S(2)}, u32[]{:S(2)}) collective-permute-start(bf16[256,64,128]{2,1,0:T(8,128)(2,1)} %get-tuple-element.8), channel_id=1, source_target_pairs={{0,4},{4,0},{1,5},{5,1},{2,6},{6,2},{3,7},{7,3},{8,12},{12,8},{9,1... | collective-permute-start | bytes 12582920 | tf_op jit(solution)/shard_map/ppermute | solution.py:211
  230.1 7.0 %collective-permute-done = bf16[256,64,128]{2,1,0:T(8,128)(2,1)S(1)} collective-permute-done((bf16[256,64,128]{2,1,0:T(8,128)(2,1)}, bf16[256,64,128]{2,1,0:T(8,128)(2,1)S(1)}, u32[]{:S(2)}, u32[]{:S(2)}) %collective-permute-start) | collective-permute-done | bytes 4194336 | tf_op jit(solution)/shard_map/ppermute | solution.py:211
  237.1 6.1 %add_convert_fusion = bf16[256,64,128]{2,1,0:T(8,128)(2,1)} fusion(bf16[256,64,128]{2,1,0:T(8,128)(2,1)S(1)} %collective-permute-done, bf16[256,64,128]{2,1,0:T(8,128)(2,1)} %get-tuple-element.7), kind=kLoop, calls=%fused_computation | loop fusion | flops 8388608 | bytes 12582912 | tf_op jit(solution)/shard_map/convert_element_type | solution.py:212
  243.2 0.0 copy-done.1
  243.2 0.0 reduce-scatter.2.cloned.1.call-update
  243.2 10.8 %shard_map.57 = f32[64,128]{1,0:T(8,128)} custom-call(s32[192]{0:T(256)} %copy-done.1, bf16[192,32,512]{2,1,0:T(8,128)(2,1)} %raw_ref.1, bf16[64,32]{1,0:T(8,128)(2,1)} %copy.13.weight_ref), custom_call_target="tpu_custom_call" | custom-call | flops 402653184 | bytes 6291456 | tf_op jit(solution)/shard_map/pallas_call | solution.py:73
  254.0 0.9 reduce_sum.28
  254.9 78.2 %psum.7 = f32[2,64]{1,0:T(2,128)S(1)} all-reduce(f32[2,64]{1,0:T(2,128)S(1)} %pad_maximum_fusion), channel_id=1, replica_groups=mesh['y'=4,'z'=8,'c'=2,'x'=4] {'y','z','c','x'}, use_global_device_ids=true, to_apply=%region_4.5 | all-reduce | flops 128 | bytes 1024 | tf_op jit(solution)/shard_map/psum | solution.py:207
  333.2 0.0 reduce-scatter.2.cloned.1.call-done
  333.2 1.2 fusion
  334.5 13.7 %all_to_all.10.part_ref = bf16[16,2,64,128]{3,2,1,0:T(8,128)(2,1)} all-to-all(bf16[16,2,64,128]{3,2,1,0:T(8,128)(2,1)S(1)} %fusion), channel_id=1, replica_groups=mesh['y'=4,'z'=8,'c'=2,'x'=4] {'x','y'}, dimensions={0} | all-to-all | bytes 1048576 | tf_op jit(solution)/shard_map/all_to_all | solution.py:217
  348.2 2.0 shard_map.58
  (6 shorter events, 0.1 us)
Async XLA Ops:
  14.0 7.9 %copy-start.5 = (u32[256]{0:T(256)S(1)}, u32[256]{0:T(256)}, u32[]{:S(2)}) copy-start(u32[256]{0:T(256)} %constant.114) | copy-start | bytes 3076
  14.0 9.1 %copy-start = (s32[192,64]{0,1:T(8,128)S(1)}, s32[192,64]{0,1:T(8,128)}, u32[]{:S(2)}) copy-start(s32[192,64]{0,1:T(8,128)} %param.7) | copy-start | bytes 147460
  14.0 9.2 %copy-start.3 = (s32[96]{0:T(128)S(1)}, s32[96]{0:T(128)}, u32[]{:S(2)}) copy-start(s32[96]{0:T(128)} %param.9) | copy-start | bytes 1156
  14.1 9.2 %copy-start.4 = (s32[96,1]{0,1:T(1,128)S(1)}, s32[96,1]{0,1:T(1,128)}, u32[]{:S(2)}) copy-start(s32[96,1]{0,1:T(1,128)} %param.8) | copy-start | bytes 1156
  14.1 160.9 %copy-start.2 = (bf16[64,32]{0,1:T(8,128)(2,1)S(1)}, bf16[64,32]{0,1:T(8,128)(2,1)}, u32[]{:S(2)}) copy-start(bf16[64,32]{0,1:T(8,128)(2,1)} %param.6) | copy-start | bytes 12292
  14.1 163.2 %all-to-all-start = ((bf16[16,48,32,128]{3,2,1,0:T(8,128)(2,1)}), bf16[16,48,32,128]{3,2,1,0:T(8,128)(2,1)}, u32[]{:S(2)}, u32[]{:S(2)}) async-start(bf16[16,48,32,128]{3,2,1,0:T(8,128)(2,1)} %bitcast.34), calls=%async_computation | async-start | bytes 12582912 | tf_op jit(solution)/shard_map/all_to_all | solution.py:202
  21.8 311.4 %reduce-scatter.2.cloned.1.call-start = ((), (), s32[]{:S(2)}) async-start(), calls=%async_computation.3 | async-start | bytes 4718592 | tf_op jit(solution)/shard_map/reduce_scatter | solution.py:213
  23.3 219.9 %copy-start.1 = (s32[192]{0:T(256)}, s32[192]{0:T(256)S(1)}, u32[]{:S(2)}) copy-start(s32[192]{0:T(256)S(1)} %get-tuple-element.10.cut_ref) | copy-start | bytes 2308
  215.2 21.9 %collective-permute-start = (bf16[256,64,128]{2,1,0:T(8,128)(2,1)}, bf16[256,64,128]{2,1,0:T(8,128)(2,1)S(1)}, u32[]{:S(2)}, u32[]{:S(2)}) collective-permute-start(bf16[256,64,128]{2,1,0:T(8,128)(2,1)} %get-tuple-element.8), channel_id=1, source_target_pairs={{0,4},{4,0},{1,5},{5,1},{2,6},{6,2},{3,7},{7,3},{8,12},{12,8},{9,1... | collective-permute-start | bytes 12582920 | tf_op jit(solution)/shard_map/ppermute | solution.py:211
Sparse Core Ops, SparseCore 0:
  243.4 53.3 reduce-scatter.1

commit v2 on v1

--- a/solution.py
+++ b/solution.py
@@ -15,36 +15,56 @@
 HALF = 64
 
 
-def pack_body(low_ref, high_ref, out_ref):
+def pack_body(note_ref, low_ref, high_ref, out_ref):
+    last = pl.program_id(0) == pl.num_programs(0) - 1
+
+    @pl.when(last)
+    def _():
+        rows, lanes = note_ref.shape
+        for dest in range(16):
+            out_ref[dest, 0, :rows] = note_ref[...]
+
+    @pl.when(jnp.logical_not(last))
+    def _():
+        pack_pairs(low_ref, high_ref, out_ref)
+
+
+def pack_pairs(low_ref, high_ref, out_ref):
     for quarter in range(4):
         for place in range(2):
             lanes = slice(quarter * LANES, (quarter + 1) * LANES)
             low = low_ref[:, place, :, lanes]
             high = high_ref[:, place, :, lanes]
-            out_ref[quarter, 2 * place] = jnp.concatenate(
+            out_ref[4 * quarter + 2 * place] = jnp.concatenate(
                 [low[..., :HALF], high[..., :HALF]], axis=-1
             )
-            out_ref[quarter, 2 * place + 1] = jnp.concatenate(
+            out_ref[4 * quarter + 2 * place + 1] = jnp.concatenate(
                 [low[..., HALF:], high[..., HALF:]], axis=-1
             )
 
 
-def packed(blocks):
+def packed(blocks, notes):
     count, _, inner, depth = blocks.shape
     pairs, step = count // 2, 8
+    steps = pairs // step
     return pl.pallas_call(
         pack_body,
-        grid=(pairs // step,),
+        grid=(steps + 1,),
         in_specs=[
-            pl.BlockSpec((step, 2, inner, depth), lambda i: (i, 0, 0, 0)),
-            pl.BlockSpec((step, 2, inner, depth), lambda i: (i + pairs // step, 0, 0, 0)),
+            pl.BlockSpec(notes.shape, lambda i: (0, 0)),
+            pl.BlockSpec(
+                (step, 2, inner, depth), lambda i: (jnp.minimum(i, steps - 1), 0, 0, 0)
+            ),
+            pl.BlockSpec(
+                (step, 2, inner, depth), lambda i: (jnp.minimum(i, steps - 1) + steps, 0, 0, 0)
+            ),
         ],
-        out_specs=pl.BlockSpec((4, 4, step, inner, LANES), lambda i: (0, 0, i, 0, 0)),
-        out_shape=jax.ShapeDtypeStruct((4, 4, pairs, inner, LANES), jnp.bfloat16),
+        out_specs=pl.BlockSpec((16, step, inner, LANES), lambda i: (0, i, 0, 0)),
+        out_shape=jax.ShapeDtypeStruct((16, pairs + 1, inner, LANES), jnp.bfloat16),
         cost_estimate=pl.CostEstimate(
             flops=4 * blocks.size, bytes_accessed=4 * blocks.size, transcendentals=0
         ),
-    )(blocks, blocks)
+    )(notes, blocks, blocks)
 
 
 def square_body(step, cut_ref, raw_ref, weight_ref, out_ref):
@@ -89,7 +109,9 @@
     return jnp.sum(lanes, axis=1)
 
 
-def stack_body(pairs, code_ref, cut_ref, raw_ref, weight_ref, mine_ref, other_ref, acc_ref):
+def stack_body(
+    pairs, code_ref, cut_ref, raw_ref, weight_ref, gain_ref, mine_ref, other_ref, acc_ref
+):
     source = pl.program_id(0)
     half = acc_ref.shape[0] // 2
 
@@ -139,8 +161,8 @@
         lax.fori_loop(0, half // 8, put, 0)
 
 
-def stacked_parts(raw, weights, codes, cuts, places):
-    sources, pairs, inner, _ = raw.shape
+def stacked_parts(raw, weights, codes, cuts, places, gain):
+    sources, pairs, inner = raw.shape[0], raw.shape[1] - 1, raw.shape[2]
     shape = (places // 2, ANG, LANES)
     return pl.pallas_call(
         functools.partial(stack_body, pairs),
@@ -150,6 +172,7 @@
             in_specs=[
                 pl.BlockSpec((1, pairs, inner, LANES), lambda i, a, b: (i, 0, 0, 0)),
                 pl.BlockSpec((ANG, inner), lambda i, a, b: (0, 0)),
+                pl.BlockSpec(memory_space=pl.ANY),
             ],
             out_specs=[pl.BlockSpec(shape, lambda i, a, b: (0, 0, 0))] * 2,
             scratch_shapes=[pltpu.VMEM((places, ANG, LANES), jnp.float32)],
@@ -161,25 +184,230 @@
         cost_estimate=pl.CostEstimate(
             flops=4 * ANG * raw.size, bytes_accessed=2 * raw.size, transcendentals=0
         ),
-    )(codes, cuts, raw, weights)
-
-
-def unpack_body(part_ref, out_ref):
+    )(codes, cuts, raw, weights, gain)
+
+
+def total_body(part_ref, out_ref, held, send_sem, recv_sem, sums):
+    x, y = lax.axis_index("x"), lax.axis_index("y")
+    z, c = lax.axis_index("z"), lax.axis_index("c")
+    flat = x * 2 + c
+
+    def near(step):
+        peer = lax.rem(flat + step, 8)
+        return {"x": peer // 2, "c": lax.rem(peer, 2)}
+
+    stages = (
+        [near(step) for step in range(1, 8)],
+        [{"y": lax.rem(y + step, 4)} for step in range(1, 4)],
+        [{"z": lax.rem(z + step, 8)} for step in range(1, 8)],
+    )
+    peers = [peer for stage in stages for peer in stage]
+    barrier = pltpu.get_barrier_semaphore()
+    for peer in peers:
+        pl.semaphore_signal(barrier, inc=1, device_id=peer, device_id_type=pl.DeviceIdType.MESH)
+    pl.semaphore_wait(barrier, len(peers))
+
+    at = 0
+    for number, stage in enumerate(stages):
+        source = part_ref if number == 0 else sums.at[number - 1]
+        copies = []
+        for peer in stage:
+            copies.append(
+                pltpu.make_async_remote_copy(
+                    src_ref=source,
+                    dst_ref=held.at[at + len(copies)],
+                    send_sem=send_sem.at[at + len(copies)],
+                    recv_sem=recv_sem.at[at + len(copies)],
+                    device_id=peer,
+                    device_id_type=pl.DeviceIdType.MESH,
+                )
+            )
+        for copy in copies:
+            copy.start()
+        for copy in copies:
+            copy.wait()
+        total = source[...]
+        for n in range(len(copies)):
+            total = total + held[at + n]
+        at += len(copies)
+        if number < 2:
+            sums[number] = total
+        else:
+            out_ref[...] = total
+
+
+def slice_total(part):
+    return pl.pallas_call(
+        total_body,
+        out_shape=jax.ShapeDtypeStruct(part.shape, jnp.float32),
+        in_specs=[pl.BlockSpec(memory_space=pltpu.VMEM)],
+        out_specs=pl.BlockSpec(memory_space=pltpu.VMEM),
+        scratch_shapes=[
+            pltpu.VMEM((17,) + part.shape, jnp.float32),
+            pltpu.SemaphoreType.DMA((17,)),
+            pltpu.SemaphoreType.DMA((17,)),
+            pltpu.VMEM((2,) + part.shape, jnp.float32),
+        ],
+        compiler_params=pltpu.CompilerParams(collective_id=1, has_side_effects=True),
+        cost_estimate=pl.CostEstimate(flops=10**9, bytes_accessed=10**6, transcendentals=0),
+    )(part)
+
+
+UP_ORDER = (2, 3, 0, 1)
+DOWN_ORDER = (0, 1, 2, 3)
+
+
+def reduce_body(
+    mine_hbm,
+    other_hbm,
+    gain_ref,
+    out_ref,
+    mine,
+    got,
+    sent,
+    came,
+    last,
+    landed,
+    load_sem,
+    swap_send,
+    swap_recv,
+    ring_send,
+    ring_recv,
+    last_send,
+    last_recv,
+):
+    x, y = lax.axis_index("x"), lax.axis_index("y")
+    z, c = lax.axis_index("z"), lax.axis_index("c")
+    ring = ({"z": lax.rem(z + 1, 8)}, {"z": lax.rem(z + 7, 8)})
+    partner = {"c": 1 - c}
+    offsets = [(dx, dy) for dx in range(4) for dy in range(4)][1:]
+    spread = [{"x": lax.rem(x + dx, 4), "y": lax.rem(y + dy, 4)} for dx, dy in offsets]
+
+    barrier = pltpu.get_barrier_semaphore()
+    peers = [partner, *ring, *spread]
+    for peer in peers:
+        pl.semaphore_signal(barrier, inc=1, device_id=peer, device_id_type=pl.DeviceIdType.MESH)
+
+    loads, swaps = {}, {}
+    for chunk in (4, 3, 5, 2, 6, 1, 7, 0):
+        loads[chunk] = pltpu.make_async_copy(
+            mine_hbm.at[chunk], mine.at[chunk], load_sem.at[chunk]
+        )
+        swaps[chunk] = pltpu.make_async_remote_copy(
+            src_ref=other_hbm.at[chunk],
+            dst_ref=got.at[chunk],
+            send_sem=swap_send.at[chunk],
+            recv_sem=swap_recv.at[chunk],
+            device_id=partner,
+            device_id_type=pl.DeviceIdType.MESH,
+        )
+    pl.semaphore_wait(barrier, len(peers))
+    for chunk in swaps:
+        swaps[chunk].start()
+        loads[chunk].start()
+
+    def own(chunk, part):
+        return mine[chunk, part].astype(jnp.float32) + got[chunk, part].astype(jnp.float32)
+
+    copies = {}
+    for step in range(4):
+        for chunk in ((4,), (3, 5), (2, 6), (1, 7))[step]:
+            loads[chunk].wait()
+            swaps[chunk].wait()
+        for turn in range(4):
+            for way, order in enumerate((UP_ORDER, DOWN_ORDER)):
+                if step == 0 and turn < 2:
+                    continue
+                part = order[turn]
+                chunk = 4 - step if way == 0 else 4 + step
+                value = own(chunk, part)
+                before = copies.get((way, step - 1, part))
+                if before is not None:
+                    before.wait_recv()
+                    value = value + came[way, step - 1, part].astype(jnp.float32)
+                sent[way, step, part] = value.astype(jnp.bfloat16)
+                copy = pltpu.make_async_remote_copy(
+                    src_ref=sent.at[way, step, part],
+                    dst_ref=came.at[way, step, part],
+                    send_sem=ring_send.at[way, step, part],
+                    recv_sem=ring_recv.at[way, step, part],
+                    device_id=ring[way],
+                    device_id_type=pl.DeviceIdType.MESH,
+                )
+                copy.start()
+                copies[way, step, part] = copy
+    loads[0].wait()
+    swaps[0].wait()
+    gain = gain_ref[...]
+    for part in (2, 0, 3, 1):
+        value = own(0, part)
+        for way in range(2):
+            copies[way, 3, part].wait_recv()
+            value = value + came[way, 3, part].astype(jnp.float32)
+        last[part] = (value * gain[None]).astype(jnp.bfloat16)
+    ends = []
+    for n, ((dx, dy), peer) in enumerate(zip(offsets, spread)):
+        copy = pltpu.make_async_remote_copy(
+            src_ref=last.at[peer["x"], pl.ds(peer["y"] * 2, 2)],
+            dst_ref=landed.at[x * 4 + y],
+            send_sem=last_send.at[n],
+            recv_sem=last_recv.at[n],
+            device_id=peer,
+            device_id_type=pl.DeviceIdType.MESH,
+        )
+        copy.start()
+        ends.append(copy)
+    landed[x * 4 + y] = last[x, pl.ds(y * 2, 2)]
+    for copy in copies.values():
+        copy.wait_send()
+    for copy in ends:
+        copy.wait()
     for quarter in range(4):
         for place in range(2):
+            rows = slice(place * ANG, (place + 1) * ANG)
+            lanes = slice(quarter * LANES, (quarter + 1) * LANES)
             for pair in range(2):
-                near = part_ref[4 * quarter + 2 * place, pair]
-                far = part_ref[4 * quarter + 2 * place + 1, pair]
-                at = (
-                    slice(place * ANG, (place + 1) * ANG),
-                    slice(quarter * LANES, (quarter + 1) * LANES),
-                )
-                out_ref[2 * pair, at[0], at[1]] = jnp.concatenate(
+                near = landed[4 * quarter + 2 * place, pair]
+                far = landed[4 * quarter + 2 * place + 1, pair]
+                out_ref[2 * pair, rows, lanes] = jnp.concatenate(
                     [near[:, :HALF], far[:, :HALF]], axis=1
                 )
-                out_ref[2 * pair + 1, at[0], at[1]] = jnp.concatenate(
+                out_ref[2 * pair + 1, rows, lanes] = jnp.concatenate(
                     [near[:, HALF:], far[:, HALF:]], axis=1
                 )
+
+
+def reduced(mine, other, gain, depth):
+    piece = (8, ANG, LANES)
+    shape = (8, 4) + piece
+    dma = pltpu.SemaphoreType.DMA
+    return pl.pallas_call(
+        reduce_body,
+        out_shape=jax.ShapeDtypeStruct((4, 2 * ANG, depth), jnp.bfloat16),
+        in_specs=[
+            pl.BlockSpec(memory_space=pl.ANY),
+            pl.BlockSpec(memory_space=pl.ANY),
+            pl.BlockSpec(memory_space=pltpu.VMEM),
+        ],
+        out_specs=pl.BlockSpec(memory_space=pltpu.VMEM),
+        scratch_shapes=[
+            pltpu.VMEM(shape, jnp.bfloat16),
+            pltpu.VMEM(shape, jnp.bfloat16),
+            pltpu.VMEM((2, 4, 4) + piece, jnp.bfloat16),
+            pltpu.VMEM((2, 4, 4) + piece, jnp.bfloat16),
+            pltpu.VMEM((4,) + piece, jnp.bfloat16),
+            pltpu.VMEM((16, 2, ANG, LANES), jnp.bfloat16),
+            dma((8,)),
+            dma((8,)),
+            dma((8,)),
+            dma((2, 4, 4)),
+            dma((2, 4, 4)),
+            dma((15,)),
+            dma((15,)),
+        ],
+        compiler_params=pltpu.CompilerParams(collective_id=2, has_side_effects=True),
+        cost_estimate=pl.CostEstimate(flops=10**9, bytes_accessed=10**7, transcendentals=0),
+    )(mine.reshape(shape), other.reshape(shape), gain)
 
 
 def local(offsets, slant_weights, live, block_tile, image_slot):
@@ -188,39 +416,28 @@
     positions, inner, depth = offsets.shape
     tile = block_tile[:, 0]
     tile_y, tile_z, tile_c = tile // 16, tile // 2 % 8, tile % 2
-    chunk = tile_z
+    chunk = (tile_z - z + 8) % 8
     place = (tile_c ^ c) * 256 + chunk * 32 + image_slot // 4 * 8 + tile_y * 2
     code = (place + image_slot // 2 % 2) * 2 + image_slot % 2
     cuts = jnp.sum(live, axis=1)
-    notes = jnp.concatenate([code, cuts])
-    notes = lax.all_gather(notes, SLAB, axis=0, tiled=False)
-    codes = notes[:, :block_count].reshape(-1)
-    own_cuts = notes[:, block_count:].reshape(-1, block_count, 2)
-    own_cuts = jnp.where(y // 2 == 0, own_cuts[..., 0], own_cuts[..., 1]).reshape(-1)
-
-    sent = packed(offsets.reshape(block_count, 2, inner, depth))
-    raw = lax.all_to_all(
-        sent.reshape((16,) + sent.shape[2:]), SLAB, split_axis=0, concat_axis=0, tiled=True
-    )
+    both_cuts = cuts.reshape(block_count, 2)
+    notes = jnp.stack([code // 32, code % 32, both_cuts[:, 0], both_cuts[:, 1]])
+    notes = jnp.pad(notes.astype(jnp.bfloat16), ((0, 12), (0, LANES - block_count)))
+
+    sent = packed(offsets.reshape(block_count, 2, inner, depth), notes)
+    got = lax.all_to_all(sent, SLAB, split_axis=0, concat_axis=0, tiled=True)
     squares = square_sums(offsets, slant_weights, cuts)
     counts = jnp.sum(live, axis=0).astype(jnp.float32)
-    totals = lax.psum(jnp.stack([squares, counts]), SHOT_GRP)
-    gain = lax.rsqrt(totals[0] / (depth * totals[1]) + 1e-06)
-
-    mine, other = stacked_parts(raw, slant_weights, codes, own_cuts, 512)
-    got = lax.ppermute(other, "c", [(0, 1), (1, 0)])
-    both = (mine.astype(jnp.float32) + got.astype(jnp.float32)).astype(jnp.bfloat16)
-    summed = lax.psum_scatter(
-        both.reshape(8, 32, ANG, LANES), "z", scatter_dimension=0, tiled=False
-    )
-    scaled = (summed.astype(jnp.float32) * gain[None, :, None]).astype(jnp.bfloat16)
-    parts = lax.all_to_all(
-        scaled.reshape(16, 2, ANG, LANES), SLAB, split_axis=0, concat_axis=0, tiled=True
-    )
-    return pl.pallas_call(
-        unpack_body,
-        out_shape=jax.ShapeDtypeStruct((4, 2 * ANG, depth), jnp.bfloat16),
-    )(parts)
+    part = jnp.pad(jnp.concatenate([squares, counts])[None], ((0, 7), (0, 0)))
+    totals = slice_total(part)[0]
+    gain = lax.rsqrt(totals[:ANG] / (depth * totals[ANG:]) + 1e-06)
+    gain = jnp.broadcast_to(gain[:, None], (ANG, LANES))
+
+    notes_in = got[:, -1, :4, :block_count].astype(jnp.int32)
+    codes = (notes_in[:, 0] * 32 + notes_in[:, 1]).reshape(-1)
+    own_cuts = jnp.where(y // 2 == 0, notes_in[:, 2], notes_in[:, 3]).reshape(-1)
+    mine, other = stacked_parts(got, slant_weights, codes, own_cuts, 512, gain)
+    return reduced(mine, other, gain, depth)
 
 
 def solution(mesh):

time: 358 us -> 244 us (0.68)
  blocking collectives: 243 us -> 0 us
  Pallas kernels: 58.3 us -> 225 us
  starting transfers between devices: 22.7 us -> 7.76 us
  between operations: 14.2 us -> 0.09 us
  waiting for transfers between devices: 7.03 us -> 0.01 us
  other arithmetic: 8.65 us -> 4.93 us
    pallas_call x2 -> x3, Pallas kernels: 9.55 us -> 176 us  [the longest x1 99.3 us: slice_total(): pl.pallas_call(total_body, out_shape=jax.ShapeDtypeStruct(part.shape, jnp...]
    unnamed x1 -> x0, blocking collectives: 151 us -> none
    psum x1 -> x0, blocking collectives: 78.2 us -> none  [local(): totals = lax.psum(jnp.stack([squares, counts]), SHOT_GRP)]
    ppermute x1 -> x0, starting transfers between devices: 14.9 us -> none  [local(): got = lax.ppermute(other, 'c', [(0, 1), (1, 0)])]
    all_to_all x1 -> x0, blocking collectives: 13.7 us -> none  [local(): lax.all_to_all(scaled.reshape(16, 2, ANG, LANES), SLAB, split_axis=0, con...]
    ppermute x1 -> x0, waiting for transfers between devices: 7 us -> none  [local(): got = lax.ppermute(other, 'c', [(0, 1), (1, 0)])]
    convert_element_type x2 -> x1, other arithmetic: 7.37 us -> 0.78 us  [local(): notes_in = got[:, -1, :4, :block_count].astype(jnp.int32)]
  transfers between devices with their start and end apart: 3 -> 1, of which waited for: 1 -> 0; matrix products, arithmetic and copies ran while one was open for 1% -> 1% of each run, Pallas kernels for 3% -> 45%
where the time goes in v2:
time: 244 us; the launch traced here: 243 us
  Pallas kernels  225 us (92%)
  starting transfers between devices  7.76 us (3%)
  local copies, waits for them, and re-layouts  5.54 us (2%)
  other arithmetic  4.93 us (2%)
    pallas_call x1, Pallas kernels, slice_total(): pl.pallas_call(total_body, out_shape=jax.ShapeDtypeStruct(part.shape, jnp...  99.3 us
    pallas_call x1, Pallas kernels, reduced(): pl.pallas_call(reduce_body, out_shape=jax.ShapeDtypeStruct((4, 2 * ANG, d...  69 us
    pallas_call x1, Pallas kernels, stacked_parts(): pl.pallas_call(functools.partial(stack_body, pairs), grid_spec=pltpu.Pref...  38 us
    pallas_call x1, Pallas kernels, square_sums(): pl.pallas_call(functools.partial(square_body, step), grid_spec=pltpu.Pref...  10.7 us
    pallas_call x1, Pallas kernels, packed(): pl.pallas_call(pack_body, grid=(steps + 1,), in_specs=[pl.BlockSpec(notes...  7.87 us
    all_to_all x1, starting transfers between devices, local(): got = lax.all_to_all(sent, SLAB, split_axis=0, concat_axis=0, tiled=True)  7.76 us
  transfers between devices with their start and end apart: 1, of which 0 were waited for; matrix products, arithmetic and copies ran while one was open for 1% of the time, Pallas kernels for 45%

profile of v2, /device:TPU:1, one launch (start us, length us, event | category | flops | bytes accessed | tf_op | source)
XLA Modules:
  0.0 243.1 jit_solution(2732675647413617023)
XLA Ops:
  0.0 0.7 convert_bitcast_fusion
  0.7 1.0 fusion.29
  1.7 0.0 copy-start.1
  1.7 0.2 reshape.49
  1.9 0.2 slice_reduce_fusion.1
  2.1 0.6 fusion.11.note_ref
  2.7 7.9 %shard_map.55 = bf16[16,49,32,128]{3,2,1,0:T(8,128)(2,1)} custom-call(bf16[16,128]{1,0:T(8,128)(2,1)} %fusion.11.note_ref, bf16[96,2,32,512]{3,2,1,0:T(8,128)(2,1)} %bitcast.37, bf16[96,2,32,512]{3,2,1,0:T(8,128)(2,1)} %bitcast.38), custom_call_target="tpu_custom_call" | custom-call | flops 12582912 | bytes 12582912 | tf_op jit(solution)/shard_map/pallas_call | solution.py:50
  10.5 0.0 copy-done.1
  10.5 0.0 copy-start
  10.5 7.8 %all-to-all-start = ((bf16[16,49,32,128]{3,2,1,0:T(8,128)(2,1)}), bf16[16,49,32,128]{3,2,1,0:T(8,128)(2,1)}, u32[]{:S(2)}, u32[]{:S(2)}) async-start(bf16[16,49,32,128]{3,2,1,0:T(8,128)(2,1)} %shard_map.55), calls=%async_computation | async-start | bytes 12845056 | tf_op jit(solution)/shard_map/all_to_all | solution.py:428
  18.3 0.0 copy-done
  18.3 0.7 copy.11.weight_ref
  19.0 10.7 %shard_map.56 = f32[64,128]{1,0:T(8,128)} custom-call(s32[192]{0:T(256)} %copy-done.1, bf16[192,32,512]{2,1,0:T(8,128)(2,1)} %raw_ref.1, bf16[64,32]{1,0:T(8,128)(2,1)} %copy.11.weight_ref), custom_call_target="tpu_custom_call" | custom-call | flops 402653184 | bytes 6291456 | tf_op jit(solution)/shard_map/pallas_call | solution.py:93
  29.7 0.9 reduce_sum.28
  30.6 0.1 maximum_bitcast_fusion
  30.7 0.6 pad.9.part_ref
  31.3 99.3 %shard_map.57 = f32[8,128]{1,0:T(8,128)} custom-call(f32[8,128]{1,0:T(8,128)} %pad.9.part_ref), custom_call_target="tpu_custom_call" | custom-call | flops 1000000000 | bytes 1000000 | tf_op jit(solution)/shard_map/pallas_call | solution.py:240
  130.6 0.8 rsqrt_bitcast_fusion
  131.4 0.0 all-to-all-done.raw_ref
  131.4 0.8 fusion
  132.2 0.1 fusion.1
  132.3 0.7 select_n.74.cut_ref
  133.0 0.7 add.85.code_ref
  133.6 0.7 broadcast_in_dim.10.gain_ref
  134.3 38.0 %shard_map.58 = (bf16[256,64,128]{2,1,0:T(8,128)(2,1)}, bf16[256,64,128]{2,1,0:T(8,128)(2,1)}) custom-call(s32[1536]{0:T(1024)} %add.85.code_ref, s32[1536]{0:T(1024)} %select_n.74.cut_ref, bf16[16,49,32,128]{3,2,1,0:T(8,128)(2,1)} %all-to-all-done.raw_ref, bf16[64,32]{1,0:T(8,128)(2,1)} %copy.11.weight_ref, f32[64,128]{1,0:T(8,128)} %broadcast_in_dim.10.gain_ref), custom_call_target="tpu_custom_call" | custom-call | flops 822083584 | bytes 6422528 | tf_op jit(solution)/shard_map/pallas_call | solution.py:167
  172.3 69.0 %shard_map.59 = bf16[4,128,512]{2,1,0:T(8,128)(2,1)} custom-call(bf16[8,4,8,64,128]{4,3,2,1,0:T(8,128)(2,1)} %bitcast.39, bf16[8,4,8,64,128]{4,3,2,1,0:T(8,128)(2,1)} %bitcast.40, f32[64,128]{1,0:T(8,128)} %broadcast_in_dim.10.gain_ref), custom_call_target="tpu_custom_call" | custom-call | flops 1000000000 | bytes 10000000 | tf_op jit(solution)/shard_map/pallas_call | solution.py:384
  241.2 1.9 copy.13
  (3 shorter events, 0.0 us)
Async XLA Ops:
  1.7 8.9 %copy-start.1 = (s32[192]{0:T(256)}, s32[192]{0:T(256)S(1)}, u32[]{:S(2)}) copy-start(s32[192]{0:T(256)S(1)} %get-tuple-element.10.cut_ref) | copy-start | bytes 2308
  10.5 7.8 %copy-start = (bf16[64,32]{0,1:T(8,128)(2,1)S(1)}, bf16[64,32]{0,1:T(8,128)(2,1)}, u32[]{:S(2)}) copy-start(bf16[64,32]{0,1:T(8,128)(2,1)} %param.6) | copy-start | bytes 12292
  10.5 120.9 %all-to-all-start = ((bf16[16,49,32,128]{3,2,1,0:T(8,128)(2,1)}), bf16[16,49,32,128]{3,2,1,0:T(8,128)(2,1)}, u32[]{:S(2)}, u32[]{:S(2)}) async-start(bf16[16,49,32,128]{3,2,1,0:T(8,128)(2,1)} %shard_map.55), calls=%async_computation | async-start | bytes 12845056 | tf_op jit(solution)/shard_map/all_to_all | solution.py:428

commit v3 on v2

v3 whole, which is shorter than its diff:
```python
import functools

import jax
import jax.numpy as jnp
from jax import lax
from jax.experimental import pallas as pl
from jax.experimental.pallas import tpu as pltpu
from jax.sharding import Mesh
from jax.sharding import PartitionSpec as P

SHOT_GRP = ("y", "z", "c", "x")
ANG = 64
LANES = 128
WAYS = 2
DEPTHS = LANES // WAYS
ROWS = ANG // WAYS
ROUND = 6
TOGETHER = 16
SOURCES = 4
MESH = pl.DeviceIdType.MESH
STEPS = (
    (1, 0), (3, 0), (0, 1), (0, 3), (1, 1), (3, 3), (1, 3), (3, 1),
    (2, 0), (0, 2), (2, 1), (1, 2), (2, 3), (3, 2), (2, 2),
)
EXACT = lax.Precision.HIGHEST


def slab_peers(x, y):
    return [{"x": lax.rem(x + dx, 4), "y": lax.rem(y + dy, 4)} for dx, dy in STEPS]


def greet(peers):
    barrier = pltpu.get_barrier_semaphore()
    for peer in peers:
        pl.semaphore_signal(barrier, inc=1, device_id=peer, device_id_type=MESH)
    pl.semaphore_wait(barrier, len(peers))


def exchange_body(
    cut_ref,
    count_ref,
    note_ref,
    weight_ref,
    offset_hbm,
    raw_hbm,
    notes_hbm,
    sums_ref,
    held,
    sent,
    load_sem,
    send_sem,
    recv_sem,
    own_sem,
    note_send,
    note_recv,
    note_own,
):
    x, y = lax.axis_index("x"), lax.axis_index("y")
    me = x * 4 + y
    peers = slab_peers(x, y)
    groups = held.shape[0] // WAYS
    rounds = groups // ROUND

    def load(turn, way):
        at = pl.ds(way * groups + turn * ROUND, ROUND)
        return pltpu.make_async_copy(offset_hbm.at[at], held.at[at], load_sem.at[turn, way])

    def start_loads(turn, carry):
        for way in range(WAYS):
            load(turn, way).start()
        return carry

    lax.fori_loop(0, rounds, start_loads, 0)
    greet(peers)

    def copy(turn, n):
        at = pl.ds(turn * ROUND, ROUND)
        peer = peers[n]
        return pltpu.make_async_remote_copy(
            src_ref=sent.at[peer["x"] * 4 + peer["y"], at],
            dst_ref=raw_hbm.at[me, at],
            send_sem=send_sem.at[turn, n],
            recv_sem=recv_sem.at[turn, n],
            device_id=peer,
            device_id_type=MESH,
        )

    def keep(turn):
        at = pl.ds(turn * ROUND, ROUND)
        return pltpu.make_async_copy(sent.at[me, at], raw_hbm.at[me, at], own_sem.at[turn])

    notes = []
    for n, peer in enumerate(peers):
        notes.append(
            pltpu.make_async_remote_copy(
                src_ref=note_ref,
                dst_ref=notes_hbm.at[me],
                send_sem=note_send.at[n],
                recv_sem=note_recv.at[n],
                device_id=peer,
                device_id_type=MESH,
            )
        )
    own_note = pltpu.make_async_copy(note_ref, notes_hbm.at[me], note_own)
    own_note.start()
    for note in notes:
        note.start()

    def send(turn, carry):
        for way in range(WAYS):
            load(turn, way).wait()
        at = pl.ds(turn * ROUND, ROUND)
        for quarter in range(4):
            lanes = slice(quarter * LANES, (quarter + 1) * LANES)
            for place in range(2):
                parts = [
                    held[pl.ds(way * groups + turn * ROUND, ROUND), place, :, lanes]
                    for way in range(WAYS)
                ]
                for end in range(2):
                    cut = slice(end * DEPTHS, (end + 1) * DEPTHS)
                    sent[4 * quarter + 2 * place + end, at] = jnp.concatenate(
                        [part[..., cut] for part in parts], axis=-1
                    )
        keep(turn).start()
        for n in range(len(peers)):
            copy(turn, n).start()
        return carry

    lax.fori_loop(0, rounds, send, 0)

    angle = lax.broadcasted_iota(jnp.int32, (ANG, LANES), 0)
    weights = weight_ref[...]

    def square(i, total):
        for place in range(2):
            angles = jnp.dot(weights, held[i, place], preferred_element_type=jnp.float32)
            squares = angles * angles
            folded = (squares[:, :128] + squares[:, 128:256]) + (
                squares[:, 256:384] + squares[:, 384:]
            )
            total = total + jnp.where(angle < cut_ref[2 * i + place], folded, 0.0)
        return total

    total = lax.fori_loop(0, held.shape[0], square, jnp.zeros((ANG, LANES), jnp.float32))
    flat = lax.dot_general(
        jnp.ones((8, LANES), jnp.float32),
        total,
        (((1,), (1,)), ((), ())),
        precision=EXACT,
        preferred_element_type=jnp.float32,
    )
    sums_ref[...] = jnp.concatenate([flat, count_ref[...]], axis=1)

    own_note.wait()
    for note in notes:
        note.wait()

    def finish(turn, carry):
        keep(turn).wait()
        for n in range(len(peers)):
            copy(turn, n).wait()
        return carry

    lax.fori_loop(0, rounds, finish, 0)


def exchanged(blocks, weights, notes, cuts, counts):
    count, _, inner, depth = blocks.shape
    groups = count // WAYS
    rounds = groups // ROUND
    dma = pltpu.SemaphoreType.DMA
    vmem = pl.BlockSpec(memory_space=pltpu.VMEM)
    return pl.pallas_call(
        exchange_body,
        out_shape=[
            jax.ShapeDtypeStruct((16, groups, inner, LANES), jnp.bfloat16),
            jax.ShapeDtypeStruct((16,) + notes.shape, jnp.bfloat16),
            jax.ShapeDtypeStruct((8, LANES), jnp.float32),
        ],
        in_specs=[
            pl.BlockSpec(memory_space=pltpu.SMEM),
            vmem,
            vmem,
            vmem,
            pl.BlockSpec(memory_space=pl.ANY),
        ],
        out_specs=[
            pl.BlockSpec(memory_space=pl.ANY),
            pl.BlockSpec(memory_space=pl.ANY),
            vmem,
        ],
        scratch_shapes=[
            pltpu.VMEM(blocks.shape, jnp.bfloat16),
            pltpu.VMEM((16, groups, inner, LANES), jnp.bfloat16),
            dma((rounds, WAYS)),
            dma((rounds, 15)),
            dma((rounds, 15)),
            dma((rounds,)),
            dma((15,)),
            dma((15,)),
            dma(()),
        ],
        compiler_params=pltpu.CompilerParams(collective_id=1, has_side_effects=True),
        cost_estimate=pl.CostEstimate(flops=10**9, bytes_accessed=10**7, transcendentals=0),
    )(cuts, counts, notes, weights, blocks)


def stack_body(
    groups, code_ref, cut_ref, raw_ref, weight_ref, mine_ref, other_ref, acc_ref, even_ref, odd_ref
):
    part = pl.program_id(0)
    half = acc_ref.shape[0] // 2
    sources, _, inner, _ = raw_ref.shape
    per_source = groups // TOGETHER
    turns = sources * per_source

    @pl.when(part == 0)
    def _():
        def clear(i, carry):
            acc_ref[pl.ds(i * 16, 16)] = jnp.zeros((16, ROWS, LANES), jnp.float32)
            return carry

        lax.fori_loop(0, acc_ref.shape[0] // 16, clear, 0)

    angle = lax.broadcasted_iota(jnp.int32, (ROWS, LANES), 0) + ROWS * (
        lax.broadcasted_iota(jnp.int32, (ROWS, LANES), 1) // DEPTHS
    )
    lane_group = lax.broadcasted_iota(jnp.int32, (inner, LANES), 1) // DEPTHS
    weights = weight_ref[...]

    def slant(turn, into_ref):
        source, first = turn // per_source, turn % per_source * TOGETHER
        tiles = []
        for u in range(TOGETHER):
            row = raw_ref[source, first + u]
            turned = [row] + [
                jnp.concatenate([row[:, t * DEPTHS :], row[:, : t * DEPTHS]], axis=1)
                for t in range(1, WAYS)
            ]
            for way in range(WAYS):
                tiles.append(
                    jnp.concatenate(
                        [
                            jnp.where(
                                lane_group == group, turned[(way - group) % WAYS], 0
                            ).astype(jnp.bfloat16)
                            for group in range(WAYS)
                        ],
                        axis=0,
                    )
                )
        angles = jnp.dot(
            weights, jnp.concatenate(tiles, axis=1), preferred_element_type=jnp.float32
        )
        for n in range(len(tiles)):
            into_ref[n] = angles[:, n * LANES : (n + 1) * LANES]

    def stack(turn, from_ref):
        source, first = turn // per_source, turn % per_source * TOGETHER
        base = (part * sources + source) * WAYS * groups + first
        places, parts = [], []
        for u in range(TOGETHER):
            for way in range(WAYS):
                at = base + way * groups + u
                places.append(code_ref[at])
                parts.append(jnp.where(angle < cut_ref[at], from_ref[u * WAYS + way], 0.0))
        for n in range(0, len(parts), 2):
            one, two = places[n], places[n + 1]
            first_sum, second_sum = acc_ref[one], acc_ref[two]
            again = jnp.where(one == two, parts[n], 0.0)
            acc_ref[one] = first_sum + parts[n]
            acc_ref[two] = (second_sum + parts[n + 1]) + again

    slant(0, even_ref)

    def step(i, carry):
        slant(2 * i + 1, odd_ref)
        stack(2 * i, even_ref)
        slant(jnp.minimum(2 * i + 2, turns - 1), even_ref)
        stack(2 * i + 1, odd_ref)
        return carry

    lax.fori_loop(0, turns // 2, step, 0)

    @pl.when(part == pl.num_programs(0) - 1)
    def _():
        def put(i, carry):
            at = pl.ds(i * 16, 16)
            mine_ref[at] = acc_ref[at].astype(mine_ref.dtype)
            other_ref[at] = acc_ref[pl.ds(half + i * 16, 16)].astype(other_ref.dtype)
            return carry

        lax.fori_loop(0, half // 16, put, 0)


def stacked_parts(raw, weights, codes, cuts, places):
    sources, groups, inner, _ = raw.shape
    shape = (places // 2, ROWS, LANES)
    buffer = pltpu.VMEM((TOGETHER * WAYS, ROWS, LANES), jnp.float32)
    return pl.pallas_call(
        functools.partial(stack_body, groups),
        grid_spec=pltpu.PrefetchScalarGridSpec(
            num_scalar_prefetch=2,
            grid=(sources // SOURCES,),
            in_specs=[
                pl.BlockSpec((SOURCES, groups, inner, LANES), lambda i, a, b: (i, 0, 0, 0)),
                pl.BlockSpec((ROWS, WAYS * inner), lambda i, a, b: (0, 0)),
            ],
            out_specs=[pl.BlockSpec(shape, lambda i, a, b: (0, 0, 0))] * 2,
            scratch_shapes=[pltpu.VMEM((places, ROWS, LANES), jnp.float32), buffer, buffer],
        ),
        out_shape=[jax.ShapeDtypeStruct(shape, jnp.bfloat16)] * 2,
        cost_estimate=pl.CostEstimate(
            flops=4 * ANG * raw.size, bytes_accessed=2 * raw.size, transcendentals=0
        ),
    )(codes, cuts, raw, weights)


UP_ORDER = (2, 3, 0, 1)
DOWN_ORDER = (0, 1, 2, 3)


def reduce_body(
    sums_ref,
    mine_hbm,
    other_hbm,
    out_ref,
    mine,
    got,
    sent,
    came,
    last,
    landed,
    sums,
    sums_in,
    load_sem,
    swap_send,
    swap_recv,
    ring_send,
    ring_recv,
    last_send,
    last_recv,
    sums_send,
    sums_recv,
):
    x, y = lax.axis_index("x"), lax.axis_index("y")
    z, c = lax.axis_index("z"), lax.axis_index("c")
    ring = ({"z": lax.rem(z + 1, 8)}, {"z": lax.rem(z + 7, 8)})
    partner = {"c": 1 - c}
    spread = slab_peers(x, y)
    column = [{"z": lax.rem(z + step, 8)} for step in range(1, 8)]
    depth = out_ref.shape[-1]

    loads, swaps = {}, {}
    for chunk in (4, 3, 5, 2, 6, 1, 7, 0):
        loads[chunk] = pltpu.make_async_copy(
            mine_hbm.at[chunk], mine.at[chunk], load_sem.at[chunk]
        )
        loads[chunk].start()
        swaps[chunk] = pltpu.make_async_remote_copy(
            src_ref=other_hbm.at[chunk],
            dst_ref=got.at[chunk],
            send_sem=swap_send.at[chunk],
            recv_sem=swap_recv.at[chunk],
            device_id=partner,
            device_id_type=MESH,
        )
    greet([partner, *column, *spread])
    for chunk in swaps:
        swaps[chunk].start()

    sum_base = (0, 1, 16)
    sum_peers = ([partner], spread, column)

    def sum_copies(stage):
        source = sums_ref if stage == 0 else sums.at[stage - 1]
        return [
            pltpu.make_async_remote_copy(
                src_ref=source,
                dst_ref=sums_in.at[sum_base[stage] + n],
                send_sem=sums_send.at[sum_base[stage] + n],
                recv_sem=sums_recv.at[sum_base[stage] + n],
                device_id=peer,
                device_id_type=MESH,
            )
            for n, peer in enumerate(sum_peers[stage])
        ]

    def sum_wait(stage, flying):
        for copy in flying:
            copy.wait()
        total = sums_ref[...] if stage == 0 else sums[stage - 1]
        for n in range(len(flying)):
            total = total + sums_in[sum_base[stage] + n]
        sums[stage] = total

    def own(chunk, part):
        return mine[chunk, part].astype(jnp.float32) + got[chunk, part].astype(jnp.float32)

    flying = sum_copies(0)
    for copy in flying:
        copy.start()
    copies = {}
    for step in range(4):
        for chunk in ((4,), (3, 5), (2, 6), (1, 7))[step]:
            loads[chunk].wait()
            swaps[chunk].wait()
        for turn in range(4):
            for way, order in enumerate((UP_ORDER, DOWN_ORDER)):
                if step == 0 and turn < 2:
                    continue
                part = order[turn]
                chunk = 4 - step if way == 0 else 4 + step
                value = own(chunk, part)
                before = copies.get((way, step - 1, part))
                if before is not None:
                    before.wait_recv()
                    value = value + came[way, step - 1, part].astype(jnp.float32)
                sent[way, step, part] = value.astype(jnp.bfloat16)
                copy = pltpu.make_async_remote_copy(
                    src_ref=sent.at[way, step, part],
                    dst_ref=came.at[way, step, part],
                    send_sem=ring_send.at[way, step, part],
                    recv_sem=ring_recv.at[way, step, part],
                    device_id=ring[way],
                    device_id_type=MESH,
                )
                copy.start()
                copies[way, step, part] = copy
        if step < 2:
            sum_wait(step, flying)
            flying = sum_copies(step + 1)
            for copy in flying:
                copy.start()
    loads[0].wait()
    swaps[0].wait()
    sum_wait(2, flying)
    totals = sums[2]
    gain = lax.rsqrt(totals[:, :ANG] / (depth * totals[:, ANG:]) + 1e-06)
    angle = lax.broadcasted_iota(jnp.int32, (ROWS, ANG), 1)
    row = lax.broadcasted_iota(jnp.int32, (ROWS, ANG), 0)
    picked = jnp.where(angle % ROWS == row, jnp.broadcast_to(gain[:1], (ROWS, ANG)), 0.0)
    angle = lax.broadcasted_iota(jnp.int32, (ANG, LANES), 0)
    lane = lax.broadcasted_iota(jnp.int32, (ANG, LANES), 1)
    chosen = jnp.where(angle // ROWS == lane // DEPTHS, 1.0, 0.0)
    gain = jnp.dot(picked, chosen, precision=EXACT, preferred_element_type=jnp.float32)
    for part in (2, 0, 3, 1):
        value = own(0, part)
        for way in range(2):
            copies[way, 3, part].wait_recv()
            value = value + came[way, 3, part].astype(jnp.float32)
        last[part] = (value * gain[None]).astype(jnp.bfloat16)
    ends = []
    for n, peer in enumerate(spread):
        copy = pltpu.make_async_remote_copy(
            src_ref=last.at[peer["x"], pl.ds(peer["y"] * 4, 4)],
            dst_ref=landed.at[x * 4 + y],
            send_sem=last_send.at[n],
            recv_sem=last_recv.at[n],
            device_id=peer,
            device_id_type=MESH,
        )
        copy.start()
        ends.append(copy)
    landed[x * 4 + y] = last[x, pl.ds(y * 4, 4)]
    for copy in copies.values():
        copy.wait_send()
    for copy in ends:
        copy.wait()
    for slot in range(4):
        for quarter in range(4):
            lanes = slice(quarter * LANES, (quarter + 1) * LANES)
            for place in range(2):
                ends_in = [landed[4 * quarter + 2 * place + end, slot] for end in range(2)]
                for group in range(WAYS):
                    at = place * ANG + group * ROWS
                    cut = slice(group * DEPTHS, (group + 1) * DEPTHS)
                    out_ref[slot, at : at + ROWS, lanes] = jnp.concatenate(
                        [part[:, cut] for part in ends_in], axis=1
                    )


def reduced(sums, mine, other, depth):
    piece = (mine.shape[0] // 32, ROWS, LANES)
    shape = (8, 4) + piece
    dma = pltpu.SemaphoreType.DMA
    vmem = pl.BlockSpec(memory_space=pltpu.VMEM)
    return pl.pallas_call(
        reduce_body,
        out_shape=jax.ShapeDtypeStruct((4, 2 * ANG, depth), jnp.bfloat16),
        in_specs=[
            vmem,
            pl.BlockSpec(memory_space=pl.ANY),
            pl.BlockSpec(memory_space=pl.ANY),
        ],
        out_specs=vmem,
        scratch_shapes=[
            pltpu.VMEM(shape, jnp.bfloat16),
            pltpu.VMEM(shape, jnp.bfloat16),
            pltpu.VMEM((2, 4, 4) + piece, jnp.bfloat16),
            pltpu.VMEM((2, 4, 4) + piece, jnp.bfloat16),
            pltpu.VMEM((4,) + piece, jnp.bfloat16),
            pltpu.VMEM((16, 4, ROWS, LANES), jnp.bfloat16),
            pltpu.VMEM((3,) + sums.shape, jnp.float32),
            pltpu.VMEM((23,) + sums.shape, jnp.float32),
            dma((8,)),
            dma((8,)),
            dma((8,)),
            dma((2, 4, 4)),
            dma((2, 4, 4)),
            dma((15,)),
            dma((15,)),
            dma((23,)),
            dma((23,)),
        ],
        compiler_params=pltpu.CompilerParams(collective_id=2, has_side_effects=True),
        cost_estimate=pl.CostEstimate(flops=10**9, bytes_accessed=10**7, transcendentals=0),
    )(sums, mine.reshape(shape), other.reshape(shape))


def local(offsets, slant_weights, live, block_tile, image_slot):
    y, z, c = lax.axis_index("y"), lax.axis_index("z"), lax.axis_index("c")
    block_count = block_tile.shape[0]
    positions, inner, depth = offsets.shape
    tile = block_tile[:, 0]
    tile_y, tile_z, tile_c = tile // 16, tile // 2 % 8, tile % 2
    chunk = (tile_z - z + 8) % 8
    code = (tile_c ^ c) * 512 + chunk * 64 + image_slot // 4 * 16 + tile_y * 4 + image_slot % 4
    cuts = jnp.sum(live, axis=1)
    both_cuts = cuts.reshape(block_count, 2)
    notes = jnp.stack([code // 32, code % 32, both_cuts[:, 0], both_cuts[:, 1]])
    notes = jnp.pad(notes.astype(jnp.bfloat16), ((0, 12), (0, LANES - block_count)))
    counts = jnp.broadcast_to(jnp.sum(live, axis=0).astype(jnp.float32)[None], (8, ANG))

    raw, notes_in, sums = exchanged(
        offsets.reshape(block_count, 2, inner, depth), slant_weights, notes, cuts, counts
    )
    notes_in = notes_in[:, :4, :block_count].astype(jnp.int32)
    codes = (notes_in[:, 0] * 32 + notes_in[:, 1]).reshape(-1)
    own_cuts = jnp.where(y // 2 == 0, notes_in[:, 2], notes_in[:, 3]).reshape(-1)
    side_by_side = slant_weights.reshape(WAYS, ROWS, inner).transpose(1, 0, 2)
    mine, other = stacked_parts(
        raw, side_by_side.reshape(ROWS, WAYS * inner), codes, own_cuts, 1024
    )
    return reduced(sums, mine, other, depth)


def solution(mesh):
    torus = Mesh(mesh.devices.reshape(4, 8, 2, mesh.shape["grp"]), SHOT_GRP)
    return jax.shard_map(
        local,
        mesh=torus,
        in_specs=(P(SHOT_GRP, None, None), P(), P(SHOT_GRP, None), P(SHOT_GRP, None), P(SHOT_GRP)),
        out_specs=P(SHOT_GRP, None, None),
        check_vma=False,
    )
```

time: 244 us -> 174 us (0.71)
  Pallas kernels: 225 us -> 164 us
  starting transfers between devices: 7.76 us -> 0 us
    pallas_call x4 -> x2, Pallas kernels: 156 us -> 98.5 us  [the longest x1 80.3 us: exchanged(): pl.pallas_call(exchange_body, out_shape=[jax.ShapeDtypeStruct((16, groups...]
    all_to_all x1 -> x0, starting transfers between devices: 7.76 us -> none  [local(): got = lax.all_to_all(sent, SLAB, split_axis=0, concat_axis=0, tiled=True)]
    pallas_call x1, Pallas kernels: 69 us -> 65.2 us  [reduced(): pl.pallas_call(reduce_body, out_shape=jax.ShapeDtypeStruct((4, 2 * ANG, d...]
  transfers between devices with their start and end apart: 1 -> 0, of which waited for: 0 -> 0; matrix products, arithmetic and copies ran while one was open for 1% -> 0% of each run, Pallas kernels for 45% -> 0%
where the time goes in v3:
time: 174 us
  Pallas kernels  164 us (94%)
  local copies, waits for them, and re-layouts  7.08 us (4%)
  other arithmetic  3.14 us (2%)
    pallas_call x1, Pallas kernels, exchanged(): pl.pallas_call(exchange_body, out_shape=[jax.ShapeDtypeStruct((16, groups...  80.3 us
    pallas_call x1, Pallas kernels, reduced(): pl.pallas_call(reduce_body, out_shape=jax.ShapeDtypeStruct((4, 2 * ANG, d...  65.2 us
    pallas_call x1, Pallas kernels, stacked_parts(): pl.pallas_call(functools.partial(stack_body, groups), grid_spec=pltpu.Pre...  18.2 us

profile of v3, /device:TPU:1, one launch (start us, length us, event | category | flops | bytes accessed | tf_op | source)
XLA Modules:
  0.0 174.0 jit_solution(2566764588345646508)
XLA Ops:
  0.0 0.7 convert_bitcast_fusion
  0.7 1.0 fusion.26
  1.7 0.0 copy-start
  1.7 0.6 broadcast_in_dim.2.count_ref
  2.3 0.8 reshape.34
  3.1 0.1 copy.11
  3.2 0.7 reshape.35.weight_ref
  3.9 1.4 copy.10.weight_ref
  5.3 0.2 reshape.38
  5.4 0.2 slice_reduce_fusion.1
  5.6 0.6 fusion.10.note_ref
  6.2 0.0 copy-done
  6.2 80.3 %shard_map.55 = (bf16[16,48,32,128]{3,2,1,0:T(8,128)(2,1)}, bf16[16,16,128]{2,1,0:T(8,128)(2,1)}, f32[8,128]{1,0:T(8,128)}) custom-call(s32[192]{0:T(256)} %copy-done, f32[8,64]{1,0:T(8,128)} %broadcast_in_dim.2.count_ref, bf16[16,128]{1,0:T(8,128)(2,1)} %fusion.10.note_ref, bf16[64,32]{1,0:T(8,128)(2,1)} %copy.10.weight_ref, bf16[96,2,32,512]{3,2,1,0:T(8,128)(2,1)} %bitcast.29), custom_call_target="tpu_custom_call" | custom-call | flops 1000000000 | bytes 10000000 | tf_op jit(solution)/shard_map/pallas_call | solution.py:174
  86.6 0.8 slice_convert_fusion
  87.3 0.1 fusion
  87.4 0.7 select_n.65.cut_ref
  88.1 0.7 add.63.code_ref
  88.7 18.2 %shard_map.56 = (bf16[512,32,128]{2,1,0:T(8,128)(2,1)}, bf16[512,32,128]{2,1,0:T(8,128)(2,1)}) custom-call(s32[1536]{0:T(1024)} %add.63.code_ref, s32[1536]{0:T(1024)} %select_n.65.cut_ref, bf16[16,48,32,128]{3,2,1,0:T(8,128)(2,1)} %get-tuple-element.12.raw_ref, bf16[32,64]{1,0:T(8,128)(2,1)} %reshape.35.weight_ref), custom_call_target="tpu_custom_call" | custom-call | flops 805306368 | bytes 6291456 | tf_op jit(solution)/shard_map/pallas_call | solution.py:301
  106.9 65.2 %shard_map.57 = bf16[4,128,512]{2,1,0:T(8,128)(2,1)} custom-call(f32[8,128]{1,0:T(8,128)} %get-tuple-element.10.sums_ref, bf16[8,4,16,32,128]{4,3,2,1,0:T(8,128)(2,1)} %bitcast.30, bf16[8,4,16,32,128]{4,3,2,1,0:T(8,128)(2,1)} %bitcast.31), custom_call_target="tpu_custom_call" | custom-call | flops 1000000000 | bytes 10000000 | tf_op jit(solution)/shard_map/pallas_call | solution.py:489
  172.1 1.9 %copy.13 = bf16[4,128,512]{2,1,0:T(8,128)(2,1)} copy(bf16[4,128,512]{2,1,0:T(8,128)(2,1)} %shard_map.57) | data formatting | bytes 1048576
  (3 shorter events, 0.0 us)
Async XLA Ops:
  1.7 4.5 %copy-start = (s32[192]{0:T(256)}, s32[192]{0:T(256)S(1)}, u32[]{:S(2)}) copy-start(s32[192]{0:T(256)S(1)} %get-tuple-element.16.cut_ref) | copy-start | bytes 2308

commit v4 on v0

v4 whole, which is shorter than its diff:
```python
import functools

import jax
import jax.numpy as jnp
from jax import lax
from jax.experimental import pallas as pl
from jax.experimental.pallas import tpu as pltpu
from jax.sharding import Mesh
from jax.sharding import PartitionSpec as P

SHOT_GRP = ("y", "z", "c", "x")
ANG = 64
LANES = 128
WAYS = 2
DEPTHS = LANES // WAYS
ROWS = ANG // WAYS
ROUND = 6
SLOTS = 16
PLACES = 1024
TILE = 256
MESH = pl.DeviceIdType.MESH
STEPS = (
    (1, 0), (3, 0), (0, 1), (0, 3), (1, 1), (3, 3), (1, 3), (3, 1),
    (2, 0), (0, 2), (2, 1), (1, 2), (2, 3), (3, 2), (2, 2),
)
UP_ORDER = (2, 3, 0, 1)
DOWN_ORDER = (0, 1, 2, 3)
EXACT = lax.Precision.HIGHEST


def exact_dot(a, b, dims):
    return lax.dot_general(
        a, b, (dims, ((), ())), precision=EXACT, preferred_element_type=jnp.float32
    )


def body(
    cut_ref,
    live_ref,
    tile_ref,
    slot_ref,
    weight_ref,
    offset_hbm,
    out_ref,
    held,
    sent,
    raw,
    acc,
    angles,
    chosen,
    cut_rows,
    even_side,
    odd_side,
    note,
    notes,
    note_sums,
    other,
    got,
    ring_out,
    ring_in,
    turned,
    last,
    landed,
    sums,
    sums_in,
    load_sem,
    send_sem,
    recv_sem,
    note_send,
    note_recv,
    swap_send,
    swap_recv,
    ring_send,
    ring_recv,
    last_send,
    last_recv,
    sums_send,
    sums_recv,
):
    x, y = lax.axis_index("x"), lax.axis_index("y")
    z, c = lax.axis_index("z"), lax.axis_index("c")
    me = x * 4 + y
    spread = [{"x": lax.rem(x + dx, 4), "y": lax.rem(y + dy, 4)} for dx, dy in STEPS]
    column = [{"z": lax.rem(z + step, 8)} for step in range(1, 8)]
    ring = (column[0], column[-1])
    partner = {"c": 1 - c}
    groups = held.shape[0] // WAYS
    rounds = groups // ROUND
    block_count, positions = tile_ref.shape[1], live_ref.shape[1]
    depth = held.shape[-1]

    def remote(source, target, send, recv, peer):
        return pltpu.make_async_remote_copy(
            src_ref=source,
            dst_ref=target,
            send_sem=send,
            recv_sem=recv,
            device_id=peer,
            device_id_type=MESH,
        )

    def load(turn, way):
        at = pl.ds(way * groups + turn * ROUND, ROUND)
        return pltpu.make_async_copy(offset_hbm.at[at], held.at[at], load_sem.at[turn, way])

    def start_loads(turn, carry):
        for way in range(WAYS):
            load(turn, way).start()
        return carry

    lax.fori_loop(0, rounds, start_loads, 0)

    tile, slot = tile_ref[...], slot_ref[...]
    code = ((tile & 1) ^ c) * 512 + ((((tile >> 1) & 7) - z + 8) & 7) * 64
    code = code + (slot >> 2) * 16 + (tile >> 4) * 4 + (slot & 3) + 1
    live = live_ref[...].astype(jnp.float32)
    position = lax.broadcasted_iota(jnp.int32, (positions, block_count), 0)
    block = lax.broadcasted_iota(jnp.int32, (positions, block_count), 1)
    live_cuts = jnp.broadcast_to(jnp.sum(live, axis=0, keepdims=True), (8, positions))
    values = [(code >> 5).astype(jnp.float32), (code & 31).astype(jnp.float32)]
    for place in range(2):
        pick = jnp.where(position == 2 * block + place, 1.0, 0.0)
        values.append(exact_dot(live_cuts, pick, ((1,), (0,)))[:1])
    turn_of = lax.broadcasted_iota(jnp.int32, (rounds, block_count), 1) % groups // ROUND
    own_turn = lax.broadcasted_iota(jnp.int32, (rounds, block_count), 0)
    spot = lax.broadcasted_iota(jnp.int32, (block_count, LANES), 0)
    lane = lax.broadcasted_iota(jnp.int32, (block_count, LANES), 1)
    spot = spot // groups * ROUND + spot % groups % ROUND + (me & 7) * SLOTS
    move = jnp.where(spot == lane, 1.0, 0.0)
    rows = [
        exact_dot(
            jnp.where(
                turn_of == own_turn, jnp.broadcast_to(value, (rounds, block_count)), 0.0
            ),
            move,
            ((1,), (0,)),
        )
        for value in values
    ]
    own_note = jnp.concatenate(rows, axis=0).astype(jnp.bfloat16)
    note[...] = own_note
    notes[me] = own_note
    weights = jnp.transpose(weight_ref[...].astype(jnp.float32)).astype(jnp.bfloat16)

    peers = [partner, *column, *spread]
    barrier = pltpu.get_barrier_semaphore()
    for peer in peers:
        pl.semaphore_signal(barrier, inc=1, device_id=peer, device_id_type=MESH)
    pl.semaphore_wait(barrier, len(peers))

    note_copies = [
        remote(note, notes.at[me], note_send.at[n], note_recv.at[n], peer)
        for n, peer in enumerate(spread)
    ]
    for copy in note_copies:
        copy.start()

    def copy(turn, n):
        at = pl.ds(turn * ROUND, ROUND)
        peer = spread[n]
        return remote(
            sent.at[peer["x"] * 4 + peer["y"], at],
            raw.at[me, at],
            send_sem.at[turn, n],
            recv_sem.at[turn, n],
            peer,
        )

    def send(turn, carry):
        for way in range(WAYS):
            load(turn, way).wait()
        at = pl.ds(turn * ROUND, ROUND)
        for quarter in range(4):
            lanes = slice(quarter * LANES, (quarter + 1) * LANES)
            for place in range(2):
                parts = [
                    held[pl.ds(way * groups + turn * ROUND, ROUND), place, :, lanes]
                    for way in range(WAYS)
                ]
                for end in range(2):
                    low = end * DEPTHS
                    sent[4 * quarter + 2 * place + end, at] = jnp.concatenate(
                        [part[..., low : low + DEPTHS] for part in parts], axis=-1
                    )
        for n in range(len(spread)):
            copy(turn, n).start()
        raw[me, at] = sent[me, at]
        return carry

    lax.fori_loop(0, rounds, send, 0)

    angle = lax.broadcasted_iota(jnp.int32, (ANG, LANES), 0)

    def square(i, total):
        for place in range(2):
            part = jnp.dot(weights, held[i, place], preferred_element_type=jnp.float32)
            squares = part * part
            folded = (squares[:, :128] + squares[:, 128:256]) + (
                squares[:, 256:384] + squares[:, 384:]
            )
            total = total + jnp.where(angle < cut_ref[2 * i + place], folded, 0.0)
        return total

    total = lax.fori_loop(0, held.shape[0], square, jnp.zeros((ANG, LANES), jnp.float32))
    along = ((1,), (1,))
    sums[0] = jnp.concatenate(
        [
            exact_dot(jnp.ones((8, LANES), jnp.float32), total, along),
            exact_dot(jnp.ones((8, positions), jnp.float32), live, along),
        ],
        axis=1,
    )
    sum_base = (0, 1, 16)
    sum_peers = ([partner], spread, column)

    def sum_start(stage):
        flying = []
        for n, peer in enumerate(sum_peers[stage], sum_base[stage]):
            flying.append(
                remote(sums.at[stage], sums_in.at[n], sums_send.at[n], sums_recv.at[n], peer)
            )
            flying[-1].start()
        return flying

    def sum_wait(stage, flying):
        for piece in flying:
            piece.wait()
        total = sums[stage]
        for n in range(len(flying)):
            total = total + sums_in[sum_base[stage] + n]
        sums[stage + 1] = total

    flying = sum_start(0)

    def clear(i, carry):
        acc[:, pl.ds(i * 8, 8)] = jnp.zeros((ROWS, 8, LANES), jnp.float32)
        return carry

    lax.fori_loop(0, PLACES // 8, clear, 0)

    def clear_angles(i, carry):
        angles[pl.ds(i * SLOTS * ROWS, SLOTS * ROWS)] = jnp.zeros(
            (SLOTS * ROWS, LANES), jnp.float32
        )
        return carry

    lax.fori_loop(0, 16, clear_angles, 0)
    sum_wait(0, flying)
    flying = sum_start(1)
    for piece in note_copies:
        piece.wait()
    for half in range(2):
        total = notes[half * 8].astype(jnp.float32)
        for n in range(1, 8):
            total = total + notes[half * 8 + n].astype(jnp.float32)
        high, low = total[:rounds], total[rounds : 2 * rounds]
        near, far = total[2 * rounds : 3 * rounds], total[3 * rounds :]
        note_sums[0, :, half * LANES : (half + 1) * LANES] = high * 32.0 + low
        note_sums[1, :, half * LANES : (half + 1) * LANES] = jnp.where(y < 2, near, far)

    low_lanes = lax.broadcasted_iota(jnp.int32, (ROWS, LANES), 1) < DEPTHS
    lane_group = lax.broadcasted_iota(jnp.int32, (TILE, LANES), 1) // DEPTHS
    together = 4

    def stack(turn, carry):
        for n in range(len(spread)):
            copy(turn, n).wait()

        def slant(i, inner_carry):
            rows = []
            for u in range(together):
                for n in range(ROUND):
                    rows.append(raw[i * together + u, turn * ROUND + n])
            part = jnp.dot(
                weights, jnp.concatenate(rows, axis=1), preferred_element_type=jnp.float32
            )
            for u in range(together):
                for n in range(ROUND):
                    at = (u * ROUND + n) * LANES
                    row = part[:, at : at + LANES]
                    swapped = pltpu.roll(row, DEPTHS, 1)
                    first = jnp.where(low_lanes, row[:ROWS], swapped[ROWS:])
                    second = jnp.where(low_lanes, swapped[:ROWS], row[ROWS:])
                    base = ((i * together + u) * SLOTS + n) * ROWS
                    angles[pl.ds(base, ROWS)] = first
                    angles[pl.ds(base + ROUND * ROWS, ROWS)] = second
            return inner_carry

        lax.fori_loop(0, 16 // together, slant, 0)

        codes = note_sums[0, pl.ds(turn, 1), :]

        def choose(i, inner_carry):
            place = lax.broadcasted_iota(jnp.int32, (64, 16 * SLOTS), 0) + (i * 64 + 1)
            same = place.astype(jnp.float32) == codes
            chosen[pl.ds(i * 64, 64)] = jnp.where(same, 1.0, 0.0).astype(jnp.bfloat16)
            return inner_carry

        lax.fori_loop(0, PLACES // 64, choose, 0)
        mark = lax.broadcasted_iota(jnp.int32, (rounds, LANES), 0) == turn
        cut = exact_dot(
            note_sums[1], jnp.where(mark, 1.0, 0.0).astype(jnp.float32), ((0,), (0,))
        )
        cut_rows[...] = cut - (lane_group * ROWS).astype(jnp.float32)

        def gather(pair, side):
            for n in range(2):
                r = 2 * pair + n
                part = angles[pl.ds(r, 16 * SLOTS, stride=ROWS), :]
                keep = cut_rows[...] > lax.convert_element_type(r, jnp.float32)
                side[:, n * LANES : (n + 1) * LANES] = jnp.where(keep, part, 0.0).astype(
                    jnp.bfloat16
                )

        def product(pair, side):
            value = side[...]
            for n in range(PLACES // TILE):
                at = pl.ds(n * TILE, TILE)
                part = jnp.dot(chosen[at], value, preferred_element_type=jnp.float32)
                acc[2 * pair, at] += part[:, :LANES]
                acc[2 * pair + 1, at] += part[:, LANES:]

        gather(0, even_side)

        def add(i, inner_carry):
            gather(2 * i + 1, odd_side)
            product(2 * i, even_side)
            gather(jnp.minimum(2 * i + 2, ROWS // 2 - 1), even_side)
            product(2 * i + 1, odd_side)
            return inner_carry

        lax.fori_loop(0, ROWS // 4, add, 0)
        return carry

    lax.fori_loop(0, rounds, stack, 0)

    swaps = {}
    for chunk in (4, 3, 5, 2, 6, 1, 7, 0):
        other[chunk] = acc[:, 512 + chunk * 64 : 512 + (chunk + 1) * 64].astype(jnp.bfloat16)
        swaps[chunk] = remote(
            other.at[chunk], got.at[chunk], swap_send.at[chunk], swap_recv.at[chunk], partner
        )
        swaps[chunk].start()
    sum_wait(1, flying)
    flying = sum_start(2)

    def own(chunk, part):
        at = chunk * 64 + part * 16
        return acc[:, at : at + 16] + got[chunk, :, part * 16 : (part + 1) * 16].astype(
            jnp.float32
        )

    copies = {}
    for step in range(4):
        for chunk in ((4,), (3, 5), (2, 6), (1, 7))[step]:
            swaps[chunk].wait()
        for number in range(4):
            for way, order in enumerate((UP_ORDER, DOWN_ORDER)):
                if step == 0 and number < 2:
                    continue
                part = order[number]
                value = own(4 - step if way == 0 else 4 + step, part)
                before = copies.get((way, step - 1, part))
                if before is not None:
                    before.wait_recv()
                    value = value + ring_in[way, step - 1, part].astype(jnp.float32)
                ring_out[way, step, part] = value.astype(jnp.bfloat16)
                piece = remote(
                    ring_out.at[way, step, part],
                    ring_in.at[way, step, part],
                    ring_send.at[way, step, part],
                    ring_recv.at[way, step, part],
                    ring[way],
                )
                piece.start()
                copies[way, step, part] = piece
    swaps[0].wait()
    sum_wait(2, flying)
    totals = sums[3]
    gain = lax.rsqrt(totals[:, :ANG] / (depth * totals[:, ANG:]) + 1e-06)
    angle = lax.broadcasted_iota(jnp.int32, (ROWS, ANG), 1)
    row = lax.broadcasted_iota(jnp.int32, (ROWS, ANG), 0)
    picked = jnp.where(angle % ROWS == row, jnp.broadcast_to(gain[:1], (ROWS, ANG)), 0.0)
    angle = lax.broadcasted_iota(jnp.int32, (ANG, LANES), 0)
    lane = lax.broadcasted_iota(jnp.int32, (ANG, LANES), 1)
    gain = exact_dot(
        picked, jnp.where(angle // ROWS == lane // DEPTHS, 1.0, 0.0), ((1,), (0,))
    )
    for part in (2, 0, 3, 1):
        value = own(0, part)
        for way in range(2):
            copies[way, 3, part].wait_recv()
            value = value + ring_in[way, 3, part].astype(jnp.float32)
        turned[...] = value.reshape(ROWS * 16, LANES)
        for n in range(16):
            rows = turned[pl.ds(n, ROWS, stride=16), :]
            last[part, n] = (rows * gain).astype(jnp.bfloat16)
    ends = []
    for n, peer in enumerate(spread):
        piece = remote(
            last.at[peer["x"], pl.ds(peer["y"] * 4, 4)],
            landed.at[me],
            last_send.at[n],
            last_recv.at[n],
            peer,
        )
        piece.start()
        ends.append(piece)
    landed[me] = last[x, pl.ds(y * 4, 4)]
    for piece in copies.values():
        piece.wait_send()
    for piece in ends:
        piece.wait()
    for slot in range(4):
        for quarter in range(4):
            lanes = slice(quarter * LANES, (quarter + 1) * LANES)
            for place in range(2):
                parts = [landed[4 * quarter + 2 * place + end, slot] for end in range(2)]
                for group in range(WAYS):
                    at = place * ANG + group * ROWS
                    cut = slice(group * DEPTHS, (group + 1) * DEPTHS)
                    out_ref[slot, at : at + ROWS, lanes] = jnp.concatenate(
                        [part[:, cut] for part in parts], axis=1
                    )


def local(offsets, slant_weights, live, block_tile, image_slot):
    block_count = block_tile.shape[0]
    positions, inner, depth = offsets.shape
    groups = block_count // WAYS
    rounds = groups // ROUND
    dma = pltpu.SemaphoreType.DMA
    vmem = pl.BlockSpec(memory_space=pltpu.VMEM)
    bf16, f32 = jnp.bfloat16, jnp.float32
    return pl.pallas_call(
        body,
        out_shape=jax.ShapeDtypeStruct((4, 2 * ANG, depth), bf16),
        in_specs=[pl.BlockSpec(memory_space=pltpu.SMEM)]
        + [vmem] * 4
        + [pl.BlockSpec(memory_space=pl.ANY)],
        out_specs=vmem,
        scratch_shapes=[
            pltpu.VMEM((block_count, 2, inner, depth), bf16),
            pltpu.VMEM((16, groups, inner, LANES), bf16),
            pltpu.VMEM((16, groups, inner, LANES), bf16),
            pltpu.VMEM((ROWS, PLACES, LANES), f32),
            pltpu.VMEM((16 * SLOTS * ROWS, LANES), f32),
            pltpu.VMEM((PLACES, 16 * SLOTS), bf16),
            pltpu.VMEM((16 * SLOTS, LANES), f32),
            pltpu.VMEM((16 * SLOTS, 2 * LANES), bf16),
            pltpu.VMEM((16 * SLOTS, 2 * LANES), bf16),
            pltpu.VMEM((4 * rounds, LANES), bf16),
            pltpu.VMEM((16, 4 * rounds, LANES), bf16),
            pltpu.VMEM((2, rounds, 16 * SLOTS), f32),
            pltpu.VMEM((8, ROWS, 64, LANES), bf16),
            pltpu.VMEM((8, ROWS, 64, LANES), bf16),
            pltpu.VMEM((2, 4, 4, ROWS, 16, LANES), bf16),
            pltpu.VMEM((2, 4, 4, ROWS, 16, LANES), bf16),
            pltpu.VMEM((ROWS * 16, LANES), f32),
            pltpu.VMEM((4, 16, ROWS, LANES), bf16),
            pltpu.VMEM((16, 4, ROWS, LANES), bf16),
            pltpu.VMEM((4, 8, LANES), f32),
            pltpu.VMEM((23, 8, LANES), f32),
            dma((rounds, WAYS)),
            dma((rounds, 15)),
            dma((rounds, 15)),
            dma((15,)),
            dma((15,)),
            dma((8,)),
            dma((8,)),
            dma((2, 4, 4)),
            dma((2, 4, 4)),
            dma((15,)),
            dma((15,)),
            dma((23,)),
            dma((23,)),
        ],
        compiler_params=pltpu.CompilerParams(
            collective_id=1, has_side_effects=True, vmem_limit_bytes=66 * 10**6
        ),
    )(
        jnp.sum(live, axis=1),
        live.T,
        block_tile.reshape(1, block_count),
        image_slot.reshape(1, block_count),
        slant_weights.T,
        offsets.reshape(block_count, 2, inner, depth),
    )


def solution(mesh):
    torus = Mesh(mesh.devices.reshape(4, 8, 2, mesh.shape["grp"]), SHOT_GRP)
    return jax.shard_map(
        local,
        mesh=torus,
        in_specs=(P(SHOT_GRP, None, None), P(), P(SHOT_GRP, None), P(SHOT_GRP, None), P(SHOT_GRP)),
        out_specs=P(SHOT_GRP, None, None),
        check_vma=False,
    )
```

time: 354 us -> 159 us (0.45)
  waiting for transfers between devices: 192 us -> 0 us
  Pallas kernels: 0 us -> 155 us
  blocking collectives: 50.8 us -> 0 us
  local copies, waits for them, and re-layouts: 46 us -> 1.87 us
  starting transfers between devices: 33.2 us -> 0 us
  matrix products: 22.7 us -> 0 us
  other arithmetic: 7.56 us -> 1.42 us
    all_to_all x4 -> x0, waiting for transfers between devices: 192 us -> none  [the longest x1 185 us: local(): lax.all_to_all(raw_sent.reshape((peer_count, capacity, 2) + inner), SHOT,...]
    pallas_call x0 -> x1, Pallas kernels: none -> 155 us  [local(): pl.pallas_call(body, out_shape=jax.ShapeDtypeStruct((4, 2 * ANG, depth),...]
    psum x4 -> x0, blocking collectives: 50.8 us -> none  [over_axes(): array = lax.psum(array, axis)]
    all_to_all x4 -> x0, starting transfers between devices: 33.2 us -> none  [the longest x1 13.1 us: local(): lax.all_to_all(labels, SHOT, split_axis=0, concat_axis=0, tiled=True)]
    dot_general x2 -> x0, matrix products: 22.7 us -> none  [the longest x1 12.7 us: slant_stack(): jnp.einsum('ah,phz->paz', weights, gathers, preferred_element_type=jnp.fl...]
    reshape x1 -> x0, local copies, waits for them, and re-layouts: 20.4 us -> none  [local(): received = angles.reshape(slot_count, traces * depth_len)]
    scatter x3 -> x0, local copies, waits for them, and re-layouts: 20 us -> none  [the longest x1 17.7 us: local(): raw_sent = jnp.zeros((slot_count, 2) + inner, jnp.bfloat16).at[targets].s...]
    broadcast_in_dim x1 -> x0, local copies, waits for them, and re-layouts: 4.29 us -> none  [local(): jnp.zeros((slot_count, 2) + inner, jnp.bfloat16).at[targets]]
  transfers between devices with their start and end apart: 4 -> 0, of which waited for: 2 -> 0; matrix products, arithmetic and copies ran while one was open for 7% -> 0% of each run, Pallas kernels for 0% -> 0%
where the time goes in v4:
time: 159 us
  Pallas kernels  155 us (97%)
  local copies, waits for them, and re-layouts  1.87 us (1%)
    pallas_call x1, Pallas kernels, local(): pl.pallas_call(body, out_shape=jax.ShapeDtypeStruct((4, 2 * ANG, depth),...  155 us

profile of v4, /device:TPU:1, one launch (start us, length us, event | category | flops | bytes accessed | tf_op | source)
XLA Modules:
  0.0 158.6 jit_solution(5504397226860758534)
XLA Ops:
  0.0 1.4 reduce_sum.9.cut_ref
  1.4 155.3 %shard_map.55 = bf16[4,128,512]{2,1,0:T(8,128)(2,1)} custom-call(s32[192]{0:T(256)} %reduce_sum.9.cut_ref, s32[64,192]{1,0:T(8,128)} %bitcast.6, s32[1,96]{1,0:T(1,128)} %bitcast.8, s32[1,96]{1,0:T(1,128)} %bitcast.9, bf16[32,64]{1,0:T(8,128)(2,1)} %bitcast.7, bf16[96,2,32,512]{3,2,1,0:T(8,128)(2,1)} %bitcast.5), custom_call_target="tpu_custom_call" | custom-call | tf_op jit(solution)/shard_map/pallas_call | solution.py:435
  156.7 1.9 %copy.7 = bf16[4,128,512]{2,1,0:T(8,128)(2,1)} copy(bf16[4,128,512]{2,1,0:T(8,128)(2,1)} %shard_map.55) | data formatting | bytes 1048576

commit v5 on v4

--- a/solution.py
+++ b/solution.py
@@ -11,11 +11,12 @@
 SHOT_GRP = ("y", "z", "c", "x")
 ANG = 64
 LANES = 128
-WAYS = 2
+WAYS = 4
 DEPTHS = LANES // WAYS
 ROWS = ANG // WAYS
-ROUND = 6
-SLOTS = 16
+ROUND = 4
+SLOTS = WAYS * ROUND
+PHASES = 2
 PLACES = 1024
 TILE = 256
 MESH = pl.DeviceIdType.MESH
@@ -121,17 +122,15 @@
     for place in range(2):
         pick = jnp.where(position == 2 * block + place, 1.0, 0.0)
         values.append(exact_dot(live_cuts, pick, ((1,), (0,)))[:1])
-    turn_of = lax.broadcasted_iota(jnp.int32, (rounds, block_count), 1) % groups // ROUND
-    own_turn = lax.broadcasted_iota(jnp.int32, (rounds, block_count), 0)
+    turn_of = lax.broadcasted_iota(jnp.int32, (8, block_count), 1) % groups // ROUND
+    own_turn = lax.broadcasted_iota(jnp.int32, (8, block_count), 0)
     spot = lax.broadcasted_iota(jnp.int32, (block_count, LANES), 0)
     lane = lax.broadcasted_iota(jnp.int32, (block_count, LANES), 1)
     spot = spot // groups * ROUND + spot % groups % ROUND + (me & 7) * SLOTS
     move = jnp.where(spot == lane, 1.0, 0.0)
     rows = [
         exact_dot(
-            jnp.where(
-                turn_of == own_turn, jnp.broadcast_to(value, (rounds, block_count)), 0.0
-            ),
+            jnp.where(turn_of == own_turn, jnp.broadcast_to(value, (8, block_count)), 0.0),
             move,
             ((1,), (0,)),
         )
@@ -155,20 +154,18 @@
     for copy in note_copies:
         copy.start()
 
-    def copy(turn, n):
+    def copy(phase, turn, n):
         at = pl.ds(turn * ROUND, ROUND)
         peer = spread[n]
         return remote(
-            sent.at[peer["x"] * 4 + peer["y"], at],
-            raw.at[me, at],
-            send_sem.at[turn, n],
-            recv_sem.at[turn, n],
+            sent.at[phase, peer["x"] * 4 + peer["y"], at],
+            raw.at[phase, me, at],
+            send_sem.at[phase, turn, n],
+            recv_sem.at[phase, turn, n],
             peer,
         )
 
-    def send(turn, carry):
-        for way in range(WAYS):
-            load(turn, way).wait()
+    def send(phase, turn):
         at = pl.ds(turn * ROUND, ROUND)
         for quarter in range(4):
             lanes = slice(quarter * LANES, (quarter + 1) * LANES)
@@ -178,16 +175,21 @@
                     for way in range(WAYS)
                 ]
                 for end in range(2):
-                    low = end * DEPTHS
-                    sent[4 * quarter + 2 * place + end, at] = jnp.concatenate(
+                    low = (end * PHASES + phase) * DEPTHS
+                    sent[phase, 4 * quarter + 2 * place + end, at] = jnp.concatenate(
                         [part[..., low : low + DEPTHS] for part in parts], axis=-1
                     )
         for n in range(len(spread)):
-            copy(turn, n).start()
-        raw[me, at] = sent[me, at]
+            copy(phase, turn, n).start()
+        raw[phase, me, at] = sent[phase, me, at]
+
+    def send_first(turn, carry):
+        for way in range(WAYS):
+            load(turn, way).wait()
+        send(0, turn)
         return carry
 
-    lax.fori_loop(0, rounds, send, 0)
+    lax.fori_loop(0, rounds, send_first, 0)
 
     angle = lax.broadcasted_iota(jnp.int32, (ANG, LANES), 0)
 
@@ -233,18 +235,11 @@
     flying = sum_start(0)
 
     def clear(i, carry):
-        acc[:, pl.ds(i * 8, 8)] = jnp.zeros((ROWS, 8, LANES), jnp.float32)
+        acc[:, :, pl.ds(i * 8, 8)] = jnp.zeros((PHASES, ROWS, 8, LANES), jnp.float32)
         return carry
 
     lax.fori_loop(0, PLACES // 8, clear, 0)
 
-    def clear_angles(i, carry):
-        angles[pl.ds(i * SLOTS * ROWS, SLOTS * ROWS)] = jnp.zeros(
-            (SLOTS * ROWS, LANES), jnp.float32
-        )
-        return carry
-
-    lax.fori_loop(0, 16, clear_angles, 0)
     sum_wait(0, flying)
     flying = sum_start(1)
     for piece in note_copies:
@@ -253,24 +248,25 @@
         total = notes[half * 8].astype(jnp.float32)
         for n in range(1, 8):
             total = total + notes[half * 8 + n].astype(jnp.float32)
-        high, low = total[:rounds], total[rounds : 2 * rounds]
-        near, far = total[2 * rounds : 3 * rounds], total[3 * rounds :]
+        high, low, near, far = total[:8], total[8:16], total[16:24], total[24:]
         note_sums[0, :, half * LANES : (half + 1) * LANES] = high * 32.0 + low
         note_sums[1, :, half * LANES : (half + 1) * LANES] = jnp.where(y < 2, near, far)
 
-    low_lanes = lax.broadcasted_iota(jnp.int32, (ROWS, LANES), 1) < DEPTHS
-    lane_group = lax.broadcasted_iota(jnp.int32, (TILE, LANES), 1) // DEPTHS
+    tile_group = lax.broadcasted_iota(jnp.int32, (ROWS, LANES), 1) // DEPTHS
+    lane_group = lax.broadcasted_iota(jnp.int32, (16 * SLOTS, LANES), 1) // DEPTHS
     together = 4
 
-    def stack(turn, carry):
+    def stack(phase, turn, carry):
         for n in range(len(spread)):
-            copy(turn, n).wait()
+            copy(phase, turn, n).wait()
+        if phase + 1 < PHASES:
+            send(phase + 1, turn)
 
         def slant(i, inner_carry):
             rows = []
             for u in range(together):
                 for n in range(ROUND):
-                    rows.append(raw[i * together + u, turn * ROUND + n])
+                    rows.append(raw[phase, i * together + u, turn * ROUND + n])
             part = jnp.dot(
                 weights, jnp.concatenate(rows, axis=1), preferred_element_type=jnp.float32
             )
@@ -278,12 +274,17 @@
                 for n in range(ROUND):
                     at = (u * ROUND + n) * LANES
                     row = part[:, at : at + LANES]
-                    swapped = pltpu.roll(row, DEPTHS, 1)
-                    first = jnp.where(low_lanes, row[:ROWS], swapped[ROWS:])
-                    second = jnp.where(low_lanes, swapped[:ROWS], row[ROWS:])
-                    base = ((i * together + u) * SLOTS + n) * ROWS
-                    angles[pl.ds(base, ROWS)] = first
-                    angles[pl.ds(base + ROUND * ROWS, ROWS)] = second
+                    moved = [row] + [
+                        pltpu.roll(row, LANES - t * DEPTHS, 1) for t in range(1, WAYS)
+                    ]
+                    for way in range(WAYS):
+                        block = moved[way][:ROWS]
+                        for group in range(1, WAYS):
+                            piece = moved[(way - group) % WAYS]
+                            piece = piece[group * ROWS : (group + 1) * ROWS]
+                            block = jnp.where(tile_group == group, piece, block)
+                        base = ((i * together + u) * SLOTS + way * ROUND + n) * ROWS
+                        angles[pl.ds(base, ROWS)] = block
             return inner_carry
 
         lax.fori_loop(0, 16 // together, slant, 0)
@@ -297,7 +298,7 @@
             return inner_carry
 
         lax.fori_loop(0, PLACES // 64, choose, 0)
-        mark = lax.broadcasted_iota(jnp.int32, (rounds, LANES), 0) == turn
+        mark = lax.broadcasted_iota(jnp.int32, (8, LANES), 0) == turn
         cut = exact_dot(
             note_sums[1], jnp.where(mark, 1.0, 0.0).astype(jnp.float32), ((0,), (0,))
         )
@@ -317,8 +318,8 @@
             for n in range(PLACES // TILE):
                 at = pl.ds(n * TILE, TILE)
                 part = jnp.dot(chosen[at], value, preferred_element_type=jnp.float32)
-                acc[2 * pair, at] += part[:, :LANES]
-                acc[2 * pair + 1, at] += part[:, LANES:]
+                acc[phase, 2 * pair, at] += part[:, :LANES]
+                acc[phase, 2 * pair + 1, at] += part[:, LANES:]
 
         gather(0, even_side)
 
@@ -332,50 +333,90 @@
         lax.fori_loop(0, ROWS // 4, add, 0)
         return carry
 
-    lax.fori_loop(0, rounds, stack, 0)
-
-    swaps = {}
-    for chunk in (4, 3, 5, 2, 6, 1, 7, 0):
-        other[chunk] = acc[:, 512 + chunk * 64 : 512 + (chunk + 1) * 64].astype(jnp.bfloat16)
-        swaps[chunk] = remote(
-            other.at[chunk], got.at[chunk], swap_send.at[chunk], swap_recv.at[chunk], partner
-        )
-        swaps[chunk].start()
-    sum_wait(1, flying)
-    flying = sum_start(2)
-
-    def own(chunk, part):
+    def run(phase, first, end):
+        lax.fori_loop(first, end, functools.partial(stack, phase), 0)
+
+    swaps, copies = {}, {}
+
+    def swap(phase):
+        for chunk in (4, 3, 5, 2, 6, 1, 7, 0):
+            half = acc[phase, :, 512 + chunk * 64 : 512 + (chunk + 1) * 64]
+            other[phase, chunk] = half.astype(jnp.bfloat16)
+            swaps[phase, chunk] = remote(
+                other.at[phase, chunk],
+                got.at[phase, chunk],
+                swap_send.at[phase, chunk],
+                swap_recv.at[phase, chunk],
+                partner,
+            )
+            swaps[phase, chunk].start()
+
+    def own(phase, chunk, part):
         at = chunk * 64 + part * 16
-        return acc[:, at : at + 16] + got[chunk, :, part * 16 : (part + 1) * 16].astype(
-            jnp.float32
-        )
-
-    copies = {}
-    for step in range(4):
+        theirs = got[phase, chunk, :, part * 16 : (part + 1) * 16]
+        return acc[phase, :, at : at + 16] + theirs.astype(jnp.float32)
+
+    def ring_step(phase, step):
         for chunk in ((4,), (3, 5), (2, 6), (1, 7))[step]:
-            swaps[chunk].wait()
+            swaps[phase, chunk].wait()
         for number in range(4):
             for way, order in enumerate((UP_ORDER, DOWN_ORDER)):
                 if step == 0 and number < 2:
                     continue
                 part = order[number]
-                value = own(4 - step if way == 0 else 4 + step, part)
-                before = copies.get((way, step - 1, part))
+                value = own(phase, 4 - step if way == 0 else 4 + step, part)
+                before = copies.get((phase, way, step - 1, part))
                 if before is not None:
                     before.wait_recv()
-                    value = value + ring_in[way, step - 1, part].astype(jnp.float32)
-                ring_out[way, step, part] = value.astype(jnp.bfloat16)
+                    value = value + ring_in[phase, way, step - 1, part].astype(jnp.float32)
+                ring_out[phase, way, step, part] = value.astype(jnp.bfloat16)
                 piece = remote(
-                    ring_out.at[way, step, part],
-                    ring_in.at[way, step, part],
-                    ring_send.at[way, step, part],
-                    ring_recv.at[way, step, part],
+                    ring_out.at[phase, way, step, part],
+                    ring_in.at[phase, way, step, part],
+                    ring_send.at[phase, way, step, part],
+                    ring_recv.at[phase, way, step, part],
                     ring[way],
                 )
                 piece.start()
-                copies[way, step, part] = piece
-    swaps[0].wait()
+                copies[phase, way, step, part] = piece
+
+    def deliver(phase, gain):
+        swaps[phase, 0].wait()
+        for part in (2, 0, 3, 1):
+            value = own(phase, 0, part)
+            for way in range(2):
+                copies[phase, way, 3, part].wait_recv()
+                value = value + ring_in[phase, way, 3, part].astype(jnp.float32)
+            turned[...] = value.reshape(ROWS * 16, LANES)
+            for n in range(16):
+                rows = turned[pl.ds(n, ROWS, stride=16), :]
+                last[phase, part, n] = (rows * gain).astype(jnp.bfloat16)
+        ends = []
+        for n, peer in enumerate(spread):
+            piece = remote(
+                last.at[phase, peer["x"], pl.ds(peer["y"] * 4, 4)],
+                landed.at[phase, me],
+                last_send.at[phase, n],
+                last_recv.at[phase, n],
+                peer,
+            )
+            piece.start()
+            ends.append(piece)
+        landed[phase, me] = last[phase, x, pl.ds(y * 4, 4)]
+        return ends
+
+    run(0, 0, rounds)
+    swap(0)
+    sum_wait(1, flying)
+    flying = sum_start(2)
+    ring_step(0, 0)
+    run(1, 0, 1)
+    ring_step(0, 1)
+    run(1, 1, 3)
+    ring_step(0, 2)
     sum_wait(2, flying)
+    run(1, 3, 4)
+    ring_step(0, 3)
     totals = sums[3]
     gain = lax.rsqrt(totals[:, :ANG] / (depth * totals[:, ANG:]) + 1e-06)
     angle = lax.broadcasted_iota(jnp.int32, (ROWS, ANG), 1)
@@ -386,27 +427,13 @@
     gain = exact_dot(
         picked, jnp.where(angle // ROWS == lane // DEPTHS, 1.0, 0.0), ((1,), (0,))
     )
-    for part in (2, 0, 3, 1):
-        value = own(0, part)
-        for way in range(2):
-            copies[way, 3, part].wait_recv()
-            value = value + ring_in[way, 3, part].astype(jnp.float32)
-        turned[...] = value.reshape(ROWS * 16, LANES)
-        for n in range(16):
-            rows = turned[pl.ds(n, ROWS, stride=16), :]
-            last[part, n] = (rows * gain).astype(jnp.bfloat16)
-    ends = []
-    for n, peer in enumerate(spread):
-        piece = remote(
-            last.at[peer["x"], pl.ds(peer["y"] * 4, 4)],
-            landed.at[me],
-            last_send.at[n],
-            last_recv.at[n],
-            peer,
-        )
-        piece.start()
-        ends.append(piece)
-    landed[me] = last[x, pl.ds(y * 4, 4)]
+    run(1, 4, 5)
+    ends = deliver(0, gain)
+    run(1, 5, rounds)
+    swap(1)
+    for step in range(4):
+        ring_step(1, step)
+    ends = ends + deliver(1, gain)
     for piece in copies.values():
         piece.wait_send()
     for piece in ends:
@@ -415,7 +442,11 @@
         for quarter in range(4):
             lanes = slice(quarter * LANES, (quarter + 1) * LANES)
             for place in range(2):
-                parts = [landed[4 * quarter + 2 * place + end, slot] for end in range(2)]
+                parts = [
+                    landed[phase, 4 * quarter + 2 * place + end, slot]
+                    for end in range(2)
+                    for phase in range(PHASES)
+                ]
                 for group in range(WAYS):
                     at = place * ANG + group * ROWS
                     cut = slice(group * DEPTHS, (group + 1) * DEPTHS)
@@ -441,37 +472,37 @@
         out_specs=vmem,
         scratch_shapes=[
             pltpu.VMEM((block_count, 2, inner, depth), bf16),
-            pltpu.VMEM((16, groups, inner, LANES), bf16),
-            pltpu.VMEM((16, groups, inner, LANES), bf16),
-            pltpu.VMEM((ROWS, PLACES, LANES), f32),
+            pltpu.VMEM((PHASES, 16, groups, inner, LANES), bf16),
+            pltpu.VMEM((PHASES, 16, groups, inner, LANES), bf16),
+            pltpu.VMEM((PHASES, ROWS, PLACES, LANES), f32),
             pltpu.VMEM((16 * SLOTS * ROWS, LANES), f32),
             pltpu.VMEM((PLACES, 16 * SLOTS), bf16),
             pltpu.VMEM((16 * SLOTS, LANES), f32),
             pltpu.VMEM((16 * SLOTS, 2 * LANES), bf16),
             pltpu.VMEM((16 * SLOTS, 2 * LANES), bf16),
-            pltpu.VMEM((4 * rounds, LANES), bf16),
-            pltpu.VMEM((16, 4 * rounds, LANES), bf16),
-            pltpu.VMEM((2, rounds, 16 * SLOTS), f32),
-            pltpu.VMEM((8, ROWS, 64, LANES), bf16),
-            pltpu.VMEM((8, ROWS, 64, LANES), bf16),
-            pltpu.VMEM((2, 4, 4, ROWS, 16, LANES), bf16),
-            pltpu.VMEM((2, 4, 4, ROWS, 16, LANES), bf16),
+            pltpu.VMEM((32, LANES), bf16),
+            pltpu.VMEM((16, 32, LANES), bf16),
+            pltpu.VMEM((2, 8, 16 * SLOTS), f32),
+            pltpu.VMEM((PHASES, 8, ROWS, 64, LANES), bf16),
+            pltpu.VMEM((PHASES, 8, ROWS, 64, LANES), bf16),
+            pltpu.VMEM((PHASES, 2, 4, 4, ROWS, 16, LANES), bf16),
+            pltpu.VMEM((PHASES, 2, 4, 4, ROWS, 16, LANES), bf16),
             pltpu.VMEM((ROWS * 16, LANES), f32),
-            pltpu.VMEM((4, 16, ROWS, LANES), bf16),
-            pltpu.VMEM((16, 4, ROWS, LANES), bf16),
+            pltpu.VMEM((PHASES, 4, 16, ROWS, LANES), bf16),
+            pltpu.VMEM((PHASES, 16, 4, ROWS, LANES), bf16),
             pltpu.VMEM((4, 8, LANES), f32),
             pltpu.VMEM((23, 8, LANES), f32),
             dma((rounds, WAYS)),
-            dma((rounds, 15)),
-            dma((rounds, 15)),
+            dma((PHASES, rounds, 15)),
+            dma((PHASES, rounds, 15)),
             dma((15,)),
             dma((15,)),
-            dma((8,)),
-            dma((8,)),
-            dma((2, 4, 4)),
-            dma((2, 4, 4)),
-            dma((15,)),
-            dma((15,)),
+            dma((PHASES, 8)),
+            dma((PHASES, 8)),
+            dma((PHASES, 2, 4, 4)),
+            dma((PHASES, 2, 4, 4)),
+            dma((PHASES, 15)),
+            dma((PHASES, 15)),
             dma((23,)),
             dma((23,)),
         ],

time: 159 us -> 147 us (0.925)
  Pallas kernels: 155 us -> 143 us
    pallas_call x1, Pallas kernels: 155 us -> 143 us  [local(): pl.pallas_call(body, out_shape=jax.ShapeDtypeStruct((4, 2 * ANG, depth),...]
where the time goes in v5:
time: 147 us
  Pallas kernels  143 us (97%)
  local copies, waits for them, and re-layouts  1.87 us (1%)
    pallas_call x1, Pallas kernels, local(): pl.pallas_call(body, out_shape=jax.ShapeDtypeStruct((4, 2 * ANG, depth),...  143 us

profile of v5, /device:TPU:1, one launch (start us, length us, event | category | flops | bytes accessed | tf_op | source)
XLA Modules:
  0.0 146.5 jit_solution(12677221562957401990)
XLA Ops:
  0.0 1.4 reduce_sum.9.cut_ref
  1.4 143.2 %shard_map.55 = bf16[4,128,512]{2,1,0:T(8,128)(2,1)} custom-call(s32[192]{0:T(256)} %reduce_sum.9.cut_ref, s32[64,192]{1,0:T(8,128)} %bitcast.6, s32[1,96]{1,0:T(1,128)} %bitcast.8, s32[1,96]{1,0:T(1,128)} %bitcast.9, bf16[32,64]{1,0:T(8,128)(2,1)} %bitcast.7, bf16[96,2,32,512]{3,2,1,0:T(8,128)(2,1)} %bitcast.5), custom_call_target="tpu_custom_call" | custom-call | tf_op jit(solution)/shard_map/pallas_call | solution.py:466
  144.6 1.9 %copy.7 = bf16[4,128,512]{2,1,0:T(8,128)(2,1)} copy(bf16[4,128,512]{2,1,0:T(8,128)(2,1)} %shard_map.55) | data formatting | bytes 1048576

commit v6 on v5

--- a/solution.py
+++ b/solution.py
@@ -252,7 +252,10 @@
         note_sums[0, :, half * LANES : (half + 1) * LANES] = high * 32.0 + low
         note_sums[1, :, half * LANES : (half + 1) * LANES] = jnp.where(y < 2, near, far)
 
-    tile_group = lax.broadcasted_iota(jnp.int32, (ROWS, LANES), 1) // DEPTHS
+    row_group = lax.broadcasted_iota(jnp.int32, (raw.shape[3], LANES), 1) // DEPTHS
+    side_by_side = jnp.concatenate(
+        [weights[group * ROWS : (group + 1) * ROWS] for group in range(WAYS)], axis=1
+    )
     lane_group = lax.broadcasted_iota(jnp.int32, (16 * SLOTS, LANES), 1) // DEPTHS
     together = 4
 
@@ -263,28 +266,30 @@
             send(phase + 1, turn)
 
         def slant(i, inner_carry):
-            rows = []
+            tiles = []
             for u in range(together):
                 for n in range(ROUND):
-                    rows.append(raw[phase, i * together + u, turn * ROUND + n])
-            part = jnp.dot(
-                weights, jnp.concatenate(rows, axis=1), preferred_element_type=jnp.float32
-            )
-            for u in range(together):
-                for n in range(ROUND):
-                    at = (u * ROUND + n) * LANES
-                    row = part[:, at : at + LANES]
+                    row = raw[phase, i * together + u, turn * ROUND + n]
                     moved = [row] + [
-                        pltpu.roll(row, LANES - t * DEPTHS, 1) for t in range(1, WAYS)
+                        jnp.concatenate([row[:, t * DEPTHS :], row[:, : t * DEPTHS]], axis=1)
+                        for t in range(1, WAYS)
                     ]
                     for way in range(WAYS):
-                        block = moved[way][:ROWS]
-                        for group in range(1, WAYS):
-                            piece = moved[(way - group) % WAYS]
-                            piece = piece[group * ROWS : (group + 1) * ROWS]
-                            block = jnp.where(tile_group == group, piece, block)
-                        base = ((i * together + u) * SLOTS + way * ROUND + n) * ROWS
-                        angles[pl.ds(base, ROWS)] = block
+                        parts = [
+                            jnp.where(row_group == group, moved[(way - group) % WAYS], 0)
+                            for group in range(WAYS)
+                        ]
+                        tiles.append(jnp.concatenate(parts, axis=0).astype(jnp.bfloat16))
+            part = jnp.dot(
+                side_by_side,
+                jnp.concatenate(tiles, axis=1),
+                preferred_element_type=jnp.float32,
+            )
+            for n in range(len(tiles)):
+                u, place = n // SLOTS, n % SLOTS
+                at = u * SLOTS + place % WAYS * ROUND + place // WAYS
+                base = (i * together * SLOTS + at) * ROWS
+                angles[pl.ds(base, ROWS)] = part[:, n * LANES : (n + 1) * LANES]
             return inner_carry
 
         lax.fori_loop(0, 16 // together, slant, 0)

time: 147 us -> 141 us (0.959)
  Pallas kernels: 143 us -> 137 us
    pallas_call x1, Pallas kernels: 143 us -> 137 us  [local(): pl.pallas_call(body, out_shape=jax.ShapeDtypeStruct((4, 2 * ANG, depth),...]
where the time goes in v6:
time: 141 us; the launch traced here: 140 us
  Pallas kernels  137 us (97%)
  local copies, waits for them, and re-layouts  1.87 us (1%)
  other arithmetic  1.42 us (1%)
    pallas_call x1, Pallas kernels, local(): pl.pallas_call(body, out_shape=jax.ShapeDtypeStruct((4, 2 * ANG, depth),...  137 us

profile of v6, /device:TPU:1, one launch (start us, length us, event | category | flops | bytes accessed | tf_op | source)
XLA Modules:
  0.0 140.5 jit_solution(8697474252637446369)
XLA Ops:
  0.0 1.4 %reduce_sum.9.cut_ref = s32[192]{0:T(256)} reduce(s32[192,64]{0,1:T(8,128)} %param.7, s32[]{:T(128)} %constant.0.clone.1), dimensions={1}, to_apply=%region_0.0 | reduce | flops 12096 | bytes 49924 | tf_op jit(solution)/shard_map/reduce_sum | solution.py:518
  1.4 137.2 %shard_map.55 = bf16[4,128,512]{2,1,0:T(8,128)(2,1)} custom-call(s32[192]{0:T(256)} %reduce_sum.9.cut_ref, s32[64,192]{1,0:T(8,128)} %bitcast.6, s32[1,96]{1,0:T(1,128)} %bitcast.8, s32[1,96]{1,0:T(1,128)} %bitcast.9, bf16[32,64]{1,0:T(8,128)(2,1)} %bitcast.7, bf16[96,2,32,512]{3,2,1,0:T(8,128)(2,1)} %bitcast.5), custom_call_target="tpu_custom_call" | custom-call | tf_op jit(solution)/shard_map/pallas_call | solution.py:471
  138.6 1.9 %copy.7 = bf16[4,128,512]{2,1,0:T(8,128)(2,1)} copy(bf16[4,128,512]{2,1,0:T(8,128)(2,1)} %shard_map.55) | data formatting | bytes 1048576
